TPU v7x, 32 devices: a whole 2x2x4 slice. The times are simulated.
32 devices in a mesh: dp: 8 (over z, y), mp: 4 (over x, core).
Axes of the slice: x: 2, y: 2, z: 4, core: 2. Of those that a mesh axis runs over, the one named last changes fastest.
Arguments:
- layer_input: bfloat16 [8, 1664, 512], P('dp'), may hold values from -6 to 6
- segments: int32 [8, 1664], P('dp'), may hold values from -1 to 12, as said below
- out_cotangent: bfloat16 [8, 1664, 512], P('dp'), may hold values from -6 to 6
- norm_gains: float32 [5, 512], replicated, may hold values from 0.5 to 1.5
- ffn1_in: bfloat16 [512, 2048], P(None, 'mp'), may hold values from -0.25 to 0.25
- ffn1_out: bfloat16 [2048, 512], P('mp'), may hold values from -0.125 to 0.125
- qkv_weight: bfloat16 [3, 512, 512], P(None, None, 'mp'), may hold values from -0.25 to 0.25
- pos_weight: bfloat16 [512, 512], P(None, 'mp'), may hold values from -0.25 to 0.25
- pos_bias: float32 [2, 512], P(None, 'mp'), may hold values from -3 to 3
- out_weight: bfloat16 [512, 512], P('mp'), may hold values from -2 to 2
- conv_in: bfloat16 [2, 512, 512], P(None, None, 'mp'), may hold values from -0.25 to 0.25
- depth_kernel: float32 [31, 512], P(None, 'mp'), may hold values from -1 to 1
- bn_scale: float32 [512], P('mp'), may hold values from 0.5 to 1.5
- bn_shift: float32 [512], P('mp'), may hold values from -3 to 3
- conv_out: bfloat16 [512, 512], P('mp'), may hold values from -0.25 to 0.25
- ffn2_in: bfloat16 [512, 2048], P(None, 'mp'), may hold values from -0.25 to 0.25
- ffn2_out: bfloat16 [2048, 512], P('mp'), may hold values from -0.125 to 0.125
Outputs:
- layer_output: bfloat16 [8, 1664, 512], P('dp')
- input_grad: bfloat16 [8, 1664, 512], P('dp')
- gains_grad: float32 [5, 512], P(None, 'dp')
- ffn1_in_grad: float32 [512, 2048], P('dp', 'mp')
- ffn1_out_grad: float32 [2048, 512], P('mp', 'dp')
- qkv_grad: float32 [3, 512, 512], P(None, 'dp', 'mp')
- pos_weight_grad: float32 [512, 512], P('dp', 'mp')
- pos_bias_grad: float32 [2, 512], P(None, 'mp')
- out_weight_grad: float32 [512, 512], P('mp', 'dp')
- conv_in_grad: float32 [2, 512, 512], P(None, 'dp', 'mp')
- kernel_grad: float32 [31, 512], P(None, 'mp')
- bn_scale_grad: float32 [512], P('mp')
- bn_shift_grad: float32 [512], P('mp')
- conv_out_grad: float32 [512, 512], P('mp', 'dp')
- ffn2_in_grad: float32 [512, 2048], P('dp', 'mp')
- ffn2_out_grad: float32 [2048, 512], P('mp', 'dp')
Inputs may be any that keep to these rules, and one draw needn't show every extreme that they name: `segments`: within a row, utterances are numbered 0, 1, 2 in frame order, each a run of consecutive frames; the frames after a row's last utterance are -1. All utterances of one row come from one bucket: from 128 to 256 frames, from 320 to 640, or from 800 to 1600. The first row begins with an utterance of exactly 1600 frames; the second row is filled with utterances of exactly 128 frames.
All inputs are finite; a program needn't handle non-finite values.
Results may differ from a plain program's by a relative error of at most 0.025.
Values may be sent and summed in bfloat16 or wider, within the bound.
A program may use at most 320 MiB of HBM per device.

v0:
```python
import math

import jax
import jax.numpy as jnp
from jax import lax
from jax.sharding import PartitionSpec as P

HEAD_DIM = 64


NORM_EPSILON = 1e-05
HIGHEST_PRECISION = lax.Precision.HIGHEST


def product(first, second):
    return jnp.dot(first, second, preferred_element_type=jnp.float32)


def left_product(first, second):
    return lax.dot_general(
        first, second, (((0,), (0,)), ((), ())), preferred_element_type=jnp.float32
    )


def right_product(first, second):
    return lax.dot_general(
        first, second, (((1,), (1,)), ((), ())), preferred_element_type=jnp.float32
    )


def swish_grad(value):
    sigmoid_out = jax.nn.sigmoid(value)
    return sigmoid_out * (1.0 + value * (1.0 - sigmoid_out))


def norm_forward(value):
    centre = value - jnp.mean(value, -1, keepdims=True)
    inverse = lax.rsqrt(jnp.mean(centre * centre, -1, keepdims=True) + NORM_EPSILON)
    return (centre * inverse, inverse)


def norm_backward(grad_out, normed, inverse, gain):
    scaled = grad_out * gain
    grad_in = inverse * (
        scaled
        - jnp.mean(scaled, -1, keepdims=True)
        - normed * jnp.mean(scaled * normed, -1, keepdims=True)
    )
    return (grad_in, jnp.sum(grad_out * normed, 0))


def rel_table(frames, features):
    count_rows = 2 * frames - 1
    distance = (jnp.arange(count_rows) - (frames - 1)).astype(jnp.float32)
    freqs = jnp.exp(
        jnp.arange(features // 2).astype(jnp.float32) * (-2.0 * math.log(10000.0) / features)
    )
    angles = distance[:, None] * freqs[None, :]
    return jnp.stack([jnp.sin(angles), jnp.cos(angles)], -1).reshape(count_rows, features)


def rel_shift(full):
    head_count, frames = (full.shape[0], full.shape[1])
    flat_rows = jnp.pad(full.reshape(head_count, frames * (2 * frames - 1)), ((0, 0), (0, frames)))
    return flat_rows.reshape(head_count, frames, 2 * frames)[:, :, :frames][:, :, ::-1]


def rel_unshift(grad_block):
    head_count, frames = (grad_block.shape[0], grad_block.shape[1])
    widened = jnp.pad(grad_block[:, :, ::-1], ((0, 0), (0, 0), (0, frames)))
    flat_rows = widened.reshape(head_count, 2 * frames * frames)[:, : frames * (2 * frames - 1)]
    return flat_rows.reshape(head_count, frames, 2 * frames - 1)


def row_scores(row_u, row_v, row_keys, pos_table, row_segment, score_scale):
    direct = jnp.einsum("ihd,jhd->hij", row_u, row_keys, preferred_element_type=jnp.float32)
    shifted = rel_shift(
        jnp.einsum("ihd,chd->hic", row_v, pos_table, preferred_element_type=jnp.float32)
    )
    matched = row_segment[:, None] == row_segment[None, :]
    return jnp.where(matched[None], (direct + shifted) * score_scale, -1e30)


def depthwise(channels, kernel, segments):
    frames = channels.shape[1]
    margin = (kernel.shape[0] - 1) // 2
    padded = jnp.pad(channels, ((0, 0), (margin, margin), (0, 0)))
    seg_pad = jnp.pad(segments, ((0, 0), (margin, margin)), constant_values=-2)
    totals = jnp.zeros_like(channels)
    for offset in range(kernel.shape[0]):
        matched = (seg_pad[:, offset : offset + frames] == segments).astype(jnp.float32)[..., None]
        totals = totals + kernel[offset] * padded[:, offset : offset + frames] * matched
    return totals


def depthwise_back(gradient, channels, kernel, segments):
    frames = channels.shape[1]
    margin = (kernel.shape[0] - 1) // 2
    padded = jnp.pad(channels, ((0, 0), (margin, margin), (0, 0)))
    seg_pad = jnp.pad(segments, ((0, 0), (margin, margin)), constant_values=-2)
    grad_pad = jnp.zeros(padded.shape, jnp.float32)
    kernel_rows = []
    for offset in range(kernel.shape[0]):
        matched = (seg_pad[:, offset : offset + frames] == segments).astype(jnp.float32)[..., None]
        masked = gradient * matched
        kernel_rows.append(jnp.sum(masked * padded[:, offset : offset + frames], (0, 1)))
        grad_pad = grad_pad.at[:, offset : offset + frames].add(kernel[offset] * masked)
    return (grad_pad[:, margin : margin + frames], jnp.stack(kernel_rows))


def ffn_forward(stream, gain, weight_in, weight_out, spread_fn, reduce_fn):
    normed, inverse = norm_forward(stream)
    hidden = spread_fn((normed * gain).astype(jnp.bfloat16))
    pre_act = product(hidden, weight_in)
    active = (pre_act * jax.nn.sigmoid(pre_act)).astype(jnp.bfloat16)
    branch = reduce_fn(product(active, weight_out))
    return (stream + 0.5 * branch, (normed, inverse, hidden, pre_act, active))


def ffn_backward(gradient, gain, weight_in, weight_out, stored, spread_fn, reduce_fn):
    normed, inverse, hidden, pre_act, active = stored
    grad_out = spread_fn((0.5 * gradient).astype(jnp.bfloat16))
    grad_pre = (right_product(grad_out, weight_out) * swish_grad(pre_act)).astype(jnp.bfloat16)
    grad_hidden = reduce_fn(right_product(grad_pre, weight_in))
    grad_stream, grad_gain = norm_backward(grad_hidden, normed, inverse, gain)
    return (
        gradient + grad_stream,
        left_product(hidden, grad_pre),
        left_product(active, grad_out),
        grad_gain,
    )


def attention_forward(stream, gain, qkv_weight, pos_weight, pos_bias, out_weight, segments):
    row_count, frames = segments.shape
    features = stream.shape[1]
    local_width = qkv_weight.shape[2]
    head_count = local_width // HEAD_DIM
    score_scale = HEAD_DIM ** (-0.5)
    normed_att, inverse_att = norm_forward(stream)
    hidden_att = (normed_att * gain).astype(jnp.bfloat16)
    queries = product(hidden_att, qkv_weight[0])
    keys_low = product(hidden_att, qkv_weight[1]).astype(jnp.bfloat16)
    values_low = product(hidden_att, qkv_weight[2]).astype(jnp.bfloat16)
    q_u = (queries + pos_bias[0]).astype(jnp.bfloat16)
    q_v = (queries + pos_bias[1]).astype(jnp.bfloat16)
    table_low = rel_table(frames, features).astype(jnp.bfloat16)
    table_heads = (
        product(table_low, pos_weight)
        .astype(jnp.bfloat16)
        .reshape(2 * frames - 1, head_count, HEAD_DIM)
    )
    shaped = (row_count, frames, head_count, HEAD_DIM)
    row_pieces = (
        q_u.reshape(shaped),
        q_v.reshape(shaped),
        keys_low.reshape(shaped),
        values_low.reshape(shaped),
        segments,
    )

    def attend(pieces):
        row_u, row_v, row_keys, row_values, row_segment = pieces
        scores = row_scores(row_u, row_v, row_keys, table_heads, row_segment, score_scale)
        row_max = jnp.max(scores, -1, keepdims=True)
        exponent = jnp.exp(scores - row_max)
        totals = jnp.sum(exponent, -1, keepdims=True)
        probability = (exponent / totals).astype(jnp.bfloat16)
        mixed_row = jnp.einsum(
            "hij,jhd->ihd", probability, row_values, preferred_element_type=jnp.float32
        )
        return (mixed_row, (row_max + jnp.log(totals))[..., 0])

    mixed, log_totals = lax.map(attend, row_pieces)
    mixed = mixed.reshape(row_count * frames, local_width).astype(jnp.bfloat16)
    kept = (
        normed_att,
        inverse_att,
        hidden_att,
        row_pieces[:4],
        log_totals,
        mixed,
        table_low,
        table_heads,
    )
    return (product(mixed, out_weight), kept)


def attention_backward(gradient, kept, qkv_weight, out_weight, segments):
    normed_att, inverse_att, hidden_att, row_parts, log_totals, mixed, table_low, table_heads = kept
    row_count, frames = segments.shape
    local_width = qkv_weight.shape[2]
    head_count = local_width // HEAD_DIM
    score_scale = HEAD_DIM ** (-0.5)
    shaped = (row_count, frames, head_count, HEAD_DIM)
    grad_att_y = gradient.astype(jnp.bfloat16)
    out_weight_g = left_product(mixed, grad_att_y)
    grad_mixed = right_product(grad_att_y, out_weight).astype(jnp.bfloat16).reshape(shaped)

    def attend_back(table_grad, pieces):
        row_u, row_v, row_keys, row_values, row_segment, row_total, row_grad = pieces
        scores = row_scores(row_u, row_v, row_keys, table_heads, row_segment, score_scale)
        probability = jnp.exp(scores - row_total[..., None])
        grad_prob = jnp.einsum(
            "ihd,jhd->hij", row_grad, row_values, preferred_element_type=jnp.float32
        )
        grad_score = (
            probability * (grad_prob - jnp.sum(grad_prob * probability, -1, keepdims=True))
        ).astype(jnp.bfloat16)
        grad_vals = jnp.einsum(
            "hij,ihd->jhd",
            probability.astype(jnp.bfloat16),
            row_grad,
            preferred_element_type=jnp.float32,
        )
        grad_u = (
            jnp.einsum("hij,jhd->ihd", grad_score, row_keys, preferred_element_type=jnp.float32)
            * score_scale
        )
        grad_k = (
            jnp.einsum("hij,ihd->jhd", grad_score, row_u, preferred_element_type=jnp.float32)
            * score_scale
        )
        grad_wide = rel_unshift(grad_score)
        grad_v = (
            jnp.einsum("hic,chd->ihd", grad_wide, table_heads, preferred_element_type=jnp.float32)
            * score_scale
        )
        table_grad = (
            table_grad
            + jnp.einsum("hic,ihd->chd", grad_wide, row_v, preferred_element_type=jnp.float32)
            * score_scale
        )
        return (table_grad, (grad_u, grad_v, grad_k, grad_vals))

    table_start = jnp.zeros((2 * frames - 1, head_count, HEAD_DIM), jnp.float32)
    table_grad, row_grads = lax.scan(
        attend_back, table_start, row_parts + (segments, log_totals, grad_mixed)
    )
    grad_u, grad_v, grad_k, grad_vals = [
        piece.reshape(row_count * frames, local_width) for piece in row_grads
    ]
    bias_grad = jnp.stack([jnp.sum(grad_u, 0), jnp.sum(grad_v, 0)])
    grad_query = (grad_u + grad_v).astype(jnp.bfloat16)
    grad_keys = grad_k.astype(jnp.bfloat16)
    grad_values = grad_vals.astype(jnp.bfloat16)
    qkv_g = jnp.stack(
        [
            left_product(hidden_att, grad_query),
            left_product(hidden_att, grad_keys),
            left_product(hidden_att, grad_values),
        ]
    )
    pos_weight_g = lax.dot_general(
        table_low.astype(jnp.float32),
        table_grad.reshape(2 * frames - 1, local_width),
        (((0,), (0,)), ((), ())),
        precision=HIGHEST_PRECISION,
        preferred_element_type=jnp.float32,
    )
    partial_hidden = (
        right_product(grad_query, qkv_weight[0])
        + right_product(grad_keys, qkv_weight[1])
        + right_product(grad_values, qkv_weight[2])
    )
    return (partial_hidden, (out_weight_g, qkv_g, pos_weight_g, bias_grad))


def conv_forward(stream, gain, conv_in, depth_kernel, bn_scale, bn_shift, conv_out, segments):
    row_count, frames = segments.shape
    local_width = conv_in.shape[2]
    normed_conv, inverse_conv = norm_forward(stream)
    hidden_conv = (normed_conv * gain).astype(jnp.bfloat16)
    glu_value = product(hidden_conv, conv_in[0])
    gate_sig = jax.nn.sigmoid(product(hidden_conv, conv_in[1]))
    channels = (glu_value * gate_sig).reshape(row_count, frames, local_width)
    filtered = depthwise(channels, depth_kernel, segments)
    valid_mask = (segments >= 0).astype(jnp.float32)[..., None]
    sum_local = jnp.sum(valid_mask * filtered, (0, 1))
    total_sum, frame_count = lax.psum((sum_local, jnp.sum(valid_mask)), "dp")
    bn_mean = total_sum / frame_count
    centred = filtered - bn_mean
    bn_var = lax.psum(jnp.sum(valid_mask * centred * centred, (0, 1)), "dp") / frame_count
    bn_rstd = lax.rsqrt(bn_var + NORM_EPSILON)
    bn_normed = centred * bn_rstd
    bn_value = bn_normed * bn_scale + bn_shift
    conv_act = (
        (bn_value * jax.nn.sigmoid(bn_value))
        .astype(jnp.bfloat16)
        .reshape(row_count * frames, local_width)
    )
    kept = (
        normed_conv,
        inverse_conv,
        hidden_conv,
        glu_value,
        gate_sig,
        channels,
        centred,
        bn_rstd,
        bn_normed,
        bn_value,
        conv_act,
        frame_count,
        valid_mask,
    )
    return (product(conv_act, conv_out), kept)


def conv_backward(gradient, kept, conv_in, depth_kernel, bn_scale, conv_out, segments):
    (
        normed_conv,
        inverse_conv,
        hidden_conv,
        glu_value,
        gate_sig,
        channels,
        centred,
        bn_rstd,
        bn_normed,
        bn_value,
        conv_act,
        frame_count,
        valid_mask,
    ) = kept
    row_count, frames = segments.shape
    local_width = conv_in.shape[2]
    grad_conv_y = gradient.astype(jnp.bfloat16)
    conv_out_g = left_product(conv_act, grad_conv_y)
    grad_act = right_product(grad_conv_y, conv_out).reshape(row_count, frames, local_width)
    grad_bn = grad_act * swish_grad(bn_value)
    shift_grad, scale_grad = lax.psum(
        (jnp.sum(grad_bn, (0, 1)), jnp.sum(grad_bn * bn_normed, (0, 1))), "dp"
    )
    grad_mean = -bn_scale * shift_grad * bn_rstd
    grad_var = -0.5 * bn_scale * scale_grad * bn_rstd * bn_rstd
    grad_filtered = (
        bn_scale * grad_bn * bn_rstd
        + valid_mask * (grad_mean + 2.0 * grad_var * centred) / frame_count
    )
    grad_channels, kernel_local = depthwise_back(grad_filtered, channels, depth_kernel, segments)
    grad_channels = grad_channels.reshape(row_count * frames, local_width)
    grad_value = (grad_channels * gate_sig).astype(jnp.bfloat16)
    grad_gate = (grad_channels * glu_value * gate_sig * (1.0 - gate_sig)).astype(jnp.bfloat16)
    conv_in_g = jnp.stack(
        [left_product(hidden_conv, grad_value), left_product(hidden_conv, grad_gate)]
    )
    partial_hidden = right_product(grad_value, conv_in[0]) + right_product(grad_gate, conv_in[1])
    return (partial_hidden, (conv_out_g, conv_in_g, kernel_local, scale_grad, shift_grad))


def per_device(
    layer_input,
    segments,
    out_cotangent,
    norm_gains,
    ffn1_in,
    ffn1_out,
    qkv_weight,
    pos_weight,
    pos_bias,
    out_weight,
    conv_in,
    depth_kernel,
    bn_scale,
    bn_shift,
    conv_out,
    ffn2_in,
    ffn2_out,
):
    row_count, frames, features = layer_input.shape
    flat_input = layer_input.astype(jnp.float32).reshape(row_count * frames, features)
    flat_grad = out_cotangent.astype(jnp.float32).reshape(row_count * frames, features)
    share_rows = row_count * frames // lax.axis_size("mp")
    share_start = lax.axis_index("mp") * share_rows

    def take_share(value):
        return lax.dynamic_slice_in_dim(value, share_start, share_rows, 0)

    def gather_stream(value):
        return lax.all_gather(value, "mp", axis=0, tiled=True)

    def scatter_branch(value):
        return lax.psum_scatter(
            value.astype(jnp.bfloat16), "mp", scatter_dimension=0, tiled=True
        ).astype(jnp.float32)

    def gather_grad(value):
        return lax.all_gather(value.astype(jnp.bfloat16), "mp", axis=0, tiled=True).astype(
            value.dtype
        )

    def scatter_back(value):
        return lax.psum_scatter(
            value.astype(jnp.bfloat16), "mp", scatter_dimension=0, tiled=True
        ).astype(jnp.float32)

    def gather_rows(value):
        return lax.all_gather(value, "mp", axis=0, tiled=True)

    def spread_rows(value):
        return lax.all_gather(value, "mp", axis=0, tiled=True)

    def reduce_rows(value):
        return lax.psum_scatter(value, "mp", scatter_dimension=0, tiled=True)

    first_in, first_out, second_in, second_out = (ffn1_in, ffn1_out, ffn2_in, ffn2_out)
    share, kept_first = ffn_forward(
        take_share(flat_input), norm_gains[0], first_in, first_out, spread_rows, reduce_rows
    )
    att_part, kept_att = attention_forward(
        gather_stream(share), norm_gains[1], qkv_weight, pos_weight, pos_bias, out_weight, segments
    )
    share = share + scatter_branch(att_part)
    conv_part, kept_conv = conv_forward(
        gather_stream(share),
        norm_gains[2],
        conv_in,
        depth_kernel,
        bn_scale,
        bn_shift,
        conv_out,
        segments,
    )
    share = share + scatter_branch(conv_part)
    share, kept_second = ffn_forward(
        share, norm_gains[3], second_in, second_out, spread_rows, reduce_rows
    )
    normed_out, inverse_out = norm_forward(share)
    layer_output = gather_rows((normed_out * norm_gains[4]).astype(jnp.bfloat16)).reshape(
        row_count, frames, features
    )
    gradient, gain_last = norm_backward(
        take_share(flat_grad), normed_out, inverse_out, norm_gains[4]
    )
    gradient, ffn2_in_g, ffn2_out_g, gain_second = ffn_backward(
        gradient, norm_gains[3], second_in, second_out, kept_second, spread_rows, reduce_rows
    )
    conv_partial, conv_grads = conv_backward(
        gather_grad(gradient), kept_conv, conv_in, depth_kernel, bn_scale, conv_out, segments
    )
    grad_stream, gain_conv = norm_backward(
        scatter_back(conv_partial),
        take_share(kept_conv[0]),
        take_share(kept_conv[1]),
        norm_gains[2],
    )
    gradient = gradient + grad_stream
    att_partial, att_grads = attention_backward(
        gather_grad(gradient), kept_att, qkv_weight, out_weight, segments
    )
    grad_stream, gain_att = norm_backward(
        scatter_back(att_partial), take_share(kept_att[0]), take_share(kept_att[1]), norm_gains[1]
    )
    gradient = gradient + grad_stream
    gradient, ffn1_in_g, ffn1_out_g, gain_first = ffn_backward(
        gradient, norm_gains[0], first_in, first_out, kept_first, spread_rows, reduce_rows
    )
    gains_local = lax.psum(
        jnp.stack([gain_first, gain_att, gain_conv, gain_second, gain_last]), "mp"
    )
    input_grad = gather_rows(gradient.astype(jnp.bfloat16)).reshape(row_count, frames, features)
    out_weight_g, qkv_g, pos_weight_g, bias_grad = att_grads
    conv_out_g, conv_in_g, kernel_local, scale_grad, shift_grad = conv_grads
    summed = (
        lax.psum_scatter(
            ffn1_in_g.astype(jnp.bfloat16), "dp", scatter_dimension=0, tiled=True
        ).astype(jnp.float32),
        lax.psum_scatter(
            ffn1_out_g.astype(jnp.bfloat16), "dp", scatter_dimension=1, tiled=True
        ).astype(jnp.float32),
        lax.psum_scatter(qkv_g.astype(jnp.bfloat16), "dp", scatter_dimension=1, tiled=True).astype(
            jnp.float32
        ),
        lax.psum_scatter(
            pos_weight_g.astype(jnp.bfloat16), "dp", scatter_dimension=0, tiled=True
        ).astype(jnp.float32),
        lax.psum_scatter(
            out_weight_g.astype(jnp.bfloat16), "dp", scatter_dimension=1, tiled=True
        ).astype(jnp.float32),
        lax.psum_scatter(
            conv_in_g.astype(jnp.bfloat16), "dp", scatter_dimension=1, tiled=True
        ).astype(jnp.float32),
        lax.psum_scatter(
            conv_out_g.astype(jnp.bfloat16), "dp", scatter_dimension=1, tiled=True
        ).astype(jnp.float32),
        lax.psum_scatter(
            ffn2_in_g.astype(jnp.bfloat16), "dp", scatter_dimension=0, tiled=True
        ).astype(jnp.float32),
        lax.psum_scatter(
            ffn2_out_g.astype(jnp.bfloat16), "dp", scatter_dimension=1, tiled=True
        ).astype(jnp.float32),
        lax.psum_scatter(
            gains_local.astype(jnp.bfloat16), "dp", scatter_dimension=1, tiled=True
        ).astype(jnp.float32),
    )
    bias_sum, kernel_sum = lax.psum((bias_grad, kernel_local), "dp")
    return (
        layer_output,
        input_grad,
        summed[9],
        summed[0],
        summed[1],
        summed[2],
        summed[3],
        bias_sum,
        summed[4],
        summed[5],
        kernel_sum,
        scale_grad,
        shift_grad,
        summed[6],
        summed[7],
        summed[8],
    )


def solution(mesh):
    placed = (
        P("dp", None, None),
        P("dp", None),
        P("dp", None, None),
        P(),
        P(None, "mp"),
        P("mp", None),
        P(None, None, "mp"),
        P(None, "mp"),
        P(None, "mp"),
        P("mp", None),
        P(None, None, "mp"),
        P(None, "mp"),
        P("mp"),
        P("mp"),
        P("mp", None),
        P(None, "mp"),
        P("mp", None),
    )
    return jax.shard_map(
        per_device,
        mesh=mesh,
        in_specs=placed,
        out_specs=(
            P("dp", None, None),
            P("dp", None, None),
            P(None, "dp"),
            P("dp", "mp"),
            P("mp", "dp"),
            P(None, "dp", "mp"),
            P("dp", "mp"),
            P(None, "mp"),
            P("mp", "dp"),
            P(None, "dp", "mp"),
            P(None, "mp"),
            P("mp"),
            P("mp"),
            P("mp", "dp"),
            P("dp", "mp"),
            P("mp", "dp"),
        ),
        check_vma=False,
    )
```

profile of v0, /device:TPU:0, one launch (start us, length us, event | category | flops | bytes accessed | tf_op | source)
XLA Modules:
  0.0 2487.6 jit_solution(16786761881394236360)
XLA Ops:
  13.9 23.2 all-gather.11.cloned.1.call-done
  46.0 39.6 %reduce-scatter.21.cloned.1.call-done = f32[416,512]{1,0:T(8,128)} async-done(((f32[1664,512]{1,0:T(8,128)}), f32[416,512]{1,0:T(8,128)}) %reduce-scatter.21.cloned.1.call-update) | async-done | bytes 851984 | tf_op jit(solution)/shard_map/reduce_scatter | solution.py:405
  88.1 97.4 %multiply_sine_fusion = (bf16[3327,256,1]{0,2,1:T(2,128)(2,1)S(1)}, bf16[3327,256,1]{0,2,1:T(2,128)(2,1)S(1)}) fusion(f32[3327]{0:T(1024)S(1)} %add_convert_fusion.5, f32[256]{0:T(256)S(1)} %multiply_exponential_fusion), kind=kLoop, calls=%fused_computation.18 | loop fusion | flops 2555136 | bytes 3421180 | tf_op jit(solution)/shard_map/sin | solution.py:59
  239.0 65.6 %reshape.1587 = f32[11072256]{0:T(1024)} reshape(f32[2,1664,3327]{2,1,0:T(8,128)} %fusion.152) | data formatting | bytes 88578048
  304.6 63.7 %reshape.1512 = f32[2,5536128]{1,0:T(2,128)} reshape(f32[11072256]{0:T(1024)} %reshape.1587) | data formatting | bytes 88578048 | tf_op jit(solution)/shard_map/while/body/eval_jaxpr/reshape | solution.py:64
  368.2 30.3 %pad.85 = f32[2,5537792]{1,0:T(2,128)} pad(f32[2,5536128]{1,0:T(2,128)} %reshape.1512, f32[]{:T(128)} %constant.941.clone.1), padding=0_0x0_1664 | pad | bytes 88591360 | tf_op jit(solution)/shard_map/while/body/eval_jaxpr/jit(_pad)/pad | solution.py:64
  398.6 35.6 %copy.60 = f32[1,2,1664,3328]{3,2,1,0:T(8,128)} copy(f32[1,2,1664,3328]{3,1,2,0:T(2,128)} %bitcast.360) | data formatting | bytes 88604672
  450.3 25.2 %copy.55 = f32[2,1664,1664]{1,2,0:T(8,128)} copy(f32[2,1664,1664]{2,1,0:T(8,128)} %slice.1304) | data formatting | bytes 44302336
  475.5 168.4 %rev.10 = f32[2,1664,1664]{1,2,0:T(8,128)} reverse(f32[2,1664,1664]{1,2,0:T(8,128)} %copy.55), dimensions={2} | reverse | bytes 44302336 | tf_op jit(solution)/shard_map/while/body/eval_jaxpr/rev | solution.py:65
  684.7 28.9 %reduce-scatter.23.cloned.1.call-done = bf16[416,512]{1,0:T(8,128)(2,1)} async-done(((bf16[1664,512]{1,0:T(8,128)(2,1)}), bf16[416,512]{1,0:T(8,128)(2,1)}) %reduce-scatter.23.cloned.1.call-update) | async-done | bytes 426000 | tf_op jit(solution)/shard_map/reduce_scatter | solution.py:384
  720.6 25.1 %all-gather.15.cloned.1.call-done = f32[1664,512]{1,0:T(8,128)} async-done(((f32[416,512]{1,0:T(8,128)}), f32[1664,512]{1,0:T(8,128)}) %all-gather.15.cloned.1.call-update) | async-done | bytes 3407888 | tf_op jit(solution)/shard_map/all_gather | solution.py:381
  766.7 22.1 all-reduce.7
  812.2 26.7 %reduce-scatter.25.cloned.1.call-done = bf16[416,512]{1,0:T(8,128)(2,1)} async-done(((bf16[1664,512]{1,0:T(8,128)(2,1)}), bf16[416,512]{1,0:T(8,128)(2,1)}) %reduce-scatter.25.cloned.1.call-update) | async-done | bytes 426000 | tf_op jit(solution)/shard_map/reduce_scatter | solution.py:384
  870.5 39.6 %reduce-scatter.27.cloned.1.call-done = f32[416,512]{1,0:T(8,128)} async-done(((f32[1664,512]{1,0:T(8,128)}), f32[416,512]{1,0:T(8,128)}) %reduce-scatter.27.cloned.1.call-update) | async-done | bytes 851984 | tf_op jit(solution)/shard_map/reduce_scatter | solution.py:405
  945.2 39.6 %reduce-scatter.29.cloned.1.call-done = f32[416,512]{1,0:T(8,128)} async-done(((f32[1664,512]{1,0:T(8,128)}), f32[416,512]{1,0:T(8,128)}) %reduce-scatter.29.cloned.1.call-update) | async-done | bytes 851984 | tf_op jit(solution)/shard_map/reduce_scatter | solution.py:405
  1189.7 24.4 reduce-scatter.31.cloned.1.call-done
  1285.2 157.4 %rev.11 = bf16[2,1664,1664]{1,2,0:T(8,128)(2,1)} reverse(bf16[2,1664,1664]{1,2,0:T(8,128)(2,1)} %multiply_convert_fusion), dimensions={2} | reverse | bytes 22151168 | tf_op jit(solution)/shard_map/while/body/eval_jaxpr/rev | solution.py:70
  1473.7 59.4 %copy.58 = bf16[1,2,1664,3328]{3,1,2,0:T(2,128)(2,1)} copy(bf16[1,2,1664,3328]{3,2,1,0:T(8,128)(2,1)S(1)} %pad_bitcast_fusion) | data formatting | bytes 44302336
  1551.8 47.7 %reshape.1589 = bf16[11072256]{0:T(1024)(128)(2,1)} reshape(bf16[2,5536128]{1,0:T(2,128)(2,1)} %slice.1335) | data formatting | bytes 44289024
  1599.5 62.6 %reshape.1520 = bf16[2,1664,3327]{2,1,0:T(8,128)(2,1)} reshape(bf16[11072256]{0:T(1024)(128)(2,1)} %reshape.1589) | data formatting | bytes 44289024 | tf_op jit(solution)/shard_map/while/body/eval_jaxpr/reshape | solution.py:72
  1683.4 28.1 %reduce-scatter.33.cloned.1.call-done = bf16[416,512]{1,0:T(8,128)(2,1)} async-done(((bf16[1664,512]{1,0:T(8,128)(2,1)}), bf16[416,512]{1,0:T(8,128)(2,1)}) %reduce-scatter.33.cloned.1.call-update) | async-done | bytes 426000 | tf_op jit(solution)/shard_map/reduce_scatter | solution.py:394
  1811.0 39.3 %reduce-scatter.53.cloned.1.call-done = bf16[512,64]{0,1:T(8,128)(2,1)} async-done(((bf16[512,512]{0,1:T(8,128)(2,1)}), bf16[512,64]{0,1:T(8,128)(2,1)}) %reduce-scatter.53.cloned.1.call-update) | async-done | bytes 65552 | tf_op jit(solution)/shard_map/reduce_scatter | solution.py:490
  1851.8 63.3 %reduce-scatter.51.cloned.1.call-done = bf16[64,512]{1,0:T(8,128)(2,1)} async-done(((bf16[512,512]{1,0:T(8,128)(2,1)}), bf16[64,512]{1,0:T(8,128)(2,1)}) %reduce-scatter.51.cloned.1.call-update) | async-done | bytes 65552 | tf_op jit(solution)/shard_map/reduce_scatter | solution.py:487
  1943.5 57.6 %reduce-scatter.49.cloned.1.call-done = bf16[128,64]{0,1:T(8,128)(2,1)} async-done(((bf16[128,512]{0,1:T(8,128)(2,1)}), bf16[128,64]{0,1:T(8,128)(2,1)}) %reduce-scatter.49.cloned.1.call-update) | async-done | bytes 16400 | tf_op jit(solution)/shard_map/reduce_scatter | solution.py:484
  2002.5 63.1 %reduce-scatter.47.cloned.1.call-done = bf16[2,64,128]{2,1,0:T(8,128)(2,1)} async-done(((bf16[2,512,128]{2,1,0:T(8,128)(2,1)}), bf16[2,64,128]{2,1,0:T(8,128)(2,1)}) %reduce-scatter.47.cloned.1.call-update) | async-done | bytes 32784 | tf_op jit(solution)/shard_map/reduce_scatter | solution.py:481
  2067.1 35.8 %all-reduce.5 = (f32[2,128]{1,0:T(2,128)}, f32[31,128]{1,0:T(8,128)}) all-reduce(f32[2,128]{1,0:T(2,128)S(1)} %pad_maximum_fusion.2, f32[31,128]{1,0:T(8,128)S(1)} %stack.204), channel_id=1, replica_groups=mesh['dp'=8,'mp'=4] {'dp'}, use_global_device_ids=true, to_apply=%region_54.55 | all-reduce | flops 4224 | bytes 33792 | tf_op jit(solution)/shard_map/psum | solution.py:497
  2102.9 27.5 %reduce-scatter.45.cloned.1.call-done = bf16[128,64]{0,1:T(8,128)(2,1)} async-done(((bf16[128,512]{0,1:T(8,128)(2,1)}), bf16[128,64]{0,1:T(8,128)(2,1)}) %reduce-scatter.45.cloned.1.call-update) | async-done | bytes 16400 | tf_op jit(solution)/shard_map/reduce_scatter | solution.py:478
  2131.7 63.5 %reduce-scatter.43.cloned.1.call-done = bf16[64,128]{1,0:T(8,128)(2,1)} async-done(((bf16[512,128]{1,0:T(8,128)(2,1)}), bf16[64,128]{1,0:T(8,128)(2,1)}) %reduce-scatter.43.cloned.1.call-update) | async-done | bytes 16400 | tf_op jit(solution)/shard_map/reduce_scatter | solution.py:475
  2196.6 63.7 %reduce-scatter.41.cloned.1.call-done = bf16[3,64,128]{2,1,0:T(8,128)(2,1)} async-done(((bf16[3,512,128]{2,1,0:T(8,128)(2,1)}), bf16[3,64,128]{2,1,0:T(8,128)(2,1)}) %reduce-scatter.41.cloned.1.call-update) | async-done | bytes 49168 | tf_op jit(solution)/shard_map/reduce_scatter | solution.py:472
  2261.7 63.5 %reduce-scatter.39.cloned.1.call-done = bf16[512,64]{0,1:T(8,128)(2,1)} async-done(((bf16[512,512]{0,1:T(8,128)(2,1)}), bf16[512,64]{0,1:T(8,128)(2,1)}) %reduce-scatter.39.cloned.1.call-update) | async-done | bytes 65552 | tf_op jit(solution)/shard_map/reduce_scatter | solution.py:469
  2326.8 63.9 %reduce-scatter.37.cloned.1.call-done = bf16[64,512]{1,0:T(8,128)(2,1)} async-done(((bf16[512,512]{1,0:T(8,128)(2,1)}), bf16[64,512]{1,0:T(8,128)(2,1)}) %reduce-scatter.37.cloned.1.call-update) | async-done | bytes 65552 | tf_op jit(solution)/shard_map/reduce_scatter | solution.py:466
  2392.1 62.6 %reduce-scatter.55.cloned.1.call-done = bf16[64,5]{1,0:T(8,128)(2,1)} async-done(((bf16[512,5]{1,0:T(8,128)(2,1)}), bf16[64,5]{1,0:T(8,128)(2,1)}) %reduce-scatter.55.cloned.1.call-update) | async-done | bytes 656
  (744 shorter events, 755.3 us)
Async XLA Ops:
  7.2 854.6 %copy-start = (bf16[512,512]{1,0:T(8,128)(2,1)S(1)}, bf16[512,512]{1,0:T(8,128)(2,1)}, u32[]{:S(2)}) copy-start(bf16[512,512]{1,0:T(8,128)(2,1)} %param.94) | copy-start | bytes 1572868
  7.2 29.9 %all-gather.11.cloned.1.call-start = ((), (), s32[]{:S(2)}) async-start(), calls=%async_computation.18 | async-start | bytes 2129920 | tf_op jit(solution)/shard_map/all_gather | solution.py:402
  13.8 71.8 %reduce-scatter.21.cloned.1.call-start = ((), (), s32[]{:S(2)}) async-start(), calls=%async_computation.19 | async-start | bytes 4259840 | tf_op jit(solution)/shard_map/reduce_scatter | solution.py:405
  46.0 163.4 %all-gather.13.cloned.1.call-start = ((), (), s32[]{:S(2)}) async-start(), calls=%async_computation.20 | async-start | bytes 4259840 | tf_op jit(solution)/shard_map/all_gather | solution.py:381
  88.0 625.5 %reduce-scatter.23.cloned.1.call-start = ((), (), s32[]{:S(2)}) async-start(), calls=%async_computation.21 | async-start | bytes 2129920 | tf_op jit(solution)/shard_map/reduce_scatter | solution.py:384
  684.6 61.2 %all-gather.15.cloned.1.call-start = ((), (), s32[]{:S(2)}) async-start(), calls=%async_computation.22 | async-start | bytes 4259840 | tf_op jit(solution)/shard_map/all_gather | solution.py:381
  715.6 123.2 %reduce-scatter.25.cloned.1.call-start = ((), (), s32[]{:S(2)}) async-start(), calls=%async_computation.23 | async-start | bytes 2129920 | tf_op jit(solution)/shard_map/reduce_scatter | solution.py:384
  718.5 359.8 %copy-start.65 = (f32[1664]{0:T(1024)}, f32[1664]{0:T(1024)S(1)}, u32[]{:S(2)}) copy-start(f32[1664]{0:T(1024)S(1)} %get-tuple-element.527) | copy-start | bytes 19972
  755.1 423.8 %copy-start.4 = (f32[1,1664,128]{2,1,0:T(8,128)}, f32[1,1664,128]{2,1,0:T(8,128)S(1)}, u32[]{:S(2)}) copy-start(f32[1,1664,128]{2,1,0:T(8,128)S(1)} %multiply_bitcast_fusion) | copy-start | bytes 2555908
  812.1 49.7 %all-gather.17.cloned.1.call-start = ((), (), s32[]{:S(2)}) async-start(), calls=%async_computation.24 | async-start | bytes 2129920 | tf_op jit(solution)/shard_map/all_gather | solution.py:402
  841.3 68.8 %reduce-scatter.27.cloned.1.call-start = ((), (), s32[]{:S(2)}) async-start(), calls=%async_computation.25 | async-start | bytes 4259840 | tf_op jit(solution)/shard_map/reduce_scatter | solution.py:405
  870.4 66.0 %all-gather.21.cloned.1.call-start = ((), (), s32[]{:S(2)}) async-start(), calls=%async_computation.27 | async-start | bytes 2129920 | tf_op jit(solution)/shard_map/all_gather | solution.py:402
  916.0 68.8 %reduce-scatter.29.cloned.1.call-start = ((), (), s32[]{:S(2)}) async-start(), calls=%async_computation.28 | async-start | bytes 4259840 | tf_op jit(solution)/shard_map/reduce_scatter | solution.py:405
  945.1 65.1 %all-gather.23.cloned.1.call-start = ((), (), s32[]{:S(2)}) async-start(), calls=%async_computation.29 | async-start | bytes 2129920 | tf_op jit(solution)/shard_map/all_gather | solution.py:389
  989.8 224.3 %reduce-scatter.31.cloned.1.call-start = ((), (), s32[]{:S(2)}) async-start(), calls=%async_computation.30 | async-start | bytes 2129920 | tf_op jit(solution)/shard_map/reduce_scatter | solution.py:394
  1188.9 50.4 %all-gather.25.cloned.1.call-start = ((), (), s32[]{:S(2)}) async-start(), calls=%async_computation.31 | async-start | bytes 2129920 | tf_op jit(solution)/shard_map/all_gather | solution.py:389
  1218.7 492.7 %reduce-scatter.33.cloned.1.call-start = ((), (), s32[]{:S(2)}) async-start(), calls=%async_computation.32 | async-start | bytes 2129920 | tf_op jit(solution)/shard_map/reduce_scatter | solution.py:394
  1266.0 414.6 %copy-start.44 = (bf16[2,64,1664]{2,1,0:T(8,128)(2,1)}, bf16[2,64,1664]{2,1,0:T(8,128)(2,1)S(1)}, u32[]{:S(2)}) copy-start(bf16[2,64,1664]{2,1,0:T(8,128)(2,1)S(1)} %fusion.13) | copy-start | bytes 1277956
  1682.5 53.8 %all-gather.27.cloned.1.call-start = ((), (), s32[]{:S(2)}) async-start(), calls=%async_computation.33 | async-start | bytes 2129920 | tf_op jit(solution)/shard_map/all_gather | solution.py:402
  1715.7 78.4 %reduce-scatter.35.cloned.1.call-start = ((), (), s32[]{:S(2)}) async-start(), calls=%async_computation.34 | async-start | bytes 4259840 | tf_op jit(solution)/shard_map/reduce_scatter | solution.py:405
  1744.7 105.6 %reduce-scatter.53.cloned.1.call-start = ((), (), s32[]{:S(2)}) async-start(), calls=%async_computation.44 | async-start | bytes 589824 | tf_op jit(solution)/shard_map/reduce_scatter | solution.py:490
  1748.9 166.3 %reduce-scatter.51.cloned.1.call-start = ((), (), s32[]{:S(2)}) async-start(), calls=%async_computation.43 | async-start | bytes 589824 | tf_op jit(solution)/shard_map/reduce_scatter | solution.py:487
  1752.7 183.3 %all-gather.19.cloned.1.call-start = ((), (), s32[]{:S(2)}) async-start(), calls=%async_computation.26 | async-start | bytes 2129920 | tf_op jit(solution)/shard_map/all_gather | solution.py:399
  1753.5 247.6 %reduce-scatter.49.cloned.1.call-start = ((), (), s32[]{:S(2)}) async-start(), calls=%async_computation.42 | async-start | bytes 147456 | tf_op jit(solution)/shard_map/reduce_scatter | solution.py:484
  1759.6 306.0 %reduce-scatter.47.cloned.1.call-start = ((), (), s32[]{:S(2)}) async-start(), calls=%async_computation.41 | async-start | bytes 294912 | tf_op jit(solution)/shard_map/reduce_scatter | solution.py:481
  1763.2 367.2 %reduce-scatter.45.cloned.1.call-start = ((), (), s32[]{:S(2)}) async-start(), calls=%async_computation.40 | async-start | bytes 147456 | tf_op jit(solution)/shard_map/reduce_scatter | solution.py:478
  1783.3 412.0 %reduce-scatter.43.cloned.1.call-start = ((), (), s32[]{:S(2)}) async-start(), calls=%async_computation.39 | async-start | bytes 147456 | tf_op jit(solution)/shard_map/reduce_scatter | solution.py:475
  1784.7 475.6 %reduce-scatter.41.cloned.1.call-start = ((), (), s32[]{:S(2)}) async-start(), calls=%async_computation.38 | async-start | bytes 442368 | tf_op jit(solution)/shard_map/reduce_scatter | solution.py:472
  1786.2 539.0 %reduce-scatter.39.cloned.1.call-start = ((), (), s32[]{:S(2)}) async-start(), calls=%async_computation.37 | async-start | bytes 589824 | tf_op jit(solution)/shard_map/reduce_scatter | solution.py:469
  1790.4 600.2 %reduce-scatter.37.cloned.1.call-start = ((), (), s32[]{:S(2)}) async-start(), calls=%async_computation.36 | async-start | bytes 589824 | tf_op jit(solution)/shard_map/reduce_scatter | solution.py:466
  1794.1 660.6 %reduce-scatter.55.cloned.1.call-start = ((), (), s32[]{:S(2)}) async-start(), calls=%async_computation.45 | async-start | bytes 147456
  1808.2 668.0 %all-gather.29.cloned.1.call-start = ((), (), s32[]{:S(2)}) async-start(), calls=%async_computation.35 | async-start | bytes 2129920 | tf_op jit(solution)/shard_map/all_gather | solution.py:399
  (232 other events, 7805.8 us)
Sparse Core Ops, SparseCore 0:
  14.0 23.0 all-gather.10
  46.1 39.5 reduce-scatter.20
  88.1 29.9 all-gather.12
  684.7 28.7 reduce-scatter.22
  715.8 29.9 all-gather.14
  812.2 26.5 reduce-scatter.24
  841.4 20.3 all-gather.16
  870.6 39.5 reduce-scatter.26
  916.1 20.3 all-gather.20
  945.2 39.5 reduce-scatter.28
  989.9 20.3 all-gather.22
  1189.0 25.1 reduce-scatter.30
  1218.8 20.3 all-gather.24
  1682.6 28.7 reduce-scatter.32
  1715.8 20.3 all-gather.26
  1744.8 39.5 reduce-scatter.34
  1787.6 62.6 reduce-scatter.52
  1853.5 61.5 reduce-scatter.50
  1916.7 19.3 all-gather.18
  1939.2 61.8 reduce-scatter.48
  2004.5 61.0 reduce-scatter.46
  2069.5 60.8 reduce-scatter.44
  2134.3 60.9 reduce-scatter.42
  2198.4 61.8 reduce-scatter.40
  2263.6 61.5 reduce-scatter.38
  2329.0 61.5 reduce-scatter.36
  2393.8 60.8 reduce-scatter.54
  2456.8 19.3 all-gather.28
where the time goes:
time: 2530 us; the launch traced here: 2490 us
  waiting for transfers between devices  986 us (39%)
  local copies, waits for them, and re-layouts  911 us (36%)
  other arithmetic  267 us (11%)
  matrix products  194 us (8%)
  blocking collectives  108 us (4%)
    unnamed x483, local copies, waits for them, and re-layouts  272 us
    rev x1, local copies, waits for them, and re-layouts, rel_shift(): flat_rows.reshape(head_count, frames, 2 * frames)[:, :, :frames][:, :, ::-1]  168 us
    rev x1, local copies, waits for them, and re-layouts, rel_unshift(): widened = jnp.pad(grad_block[:, :, ::-1], ((0, 0), (0, 0), (0, frames)))  157 us
    reduce_scatter x4, waiting for transfers between devices, reduce_rows(): return lax.psum_scatter(value, 'mp', scatter_dimension=0, tiled=True)  119 us
    scatter-add x28, local copies, waits for them, and re-layouts, depthwise_back(): grad_pad.at[:, offset:offset + frames].add(kernel[offset] * masked)  109 us
    sin x1, other arithmetic, rel_table(): jnp.sin(angles)  97.4 us
    all_gather x4, waiting for transfers between devices, spread_rows(): return lax.all_gather(value, 'mp', axis=0, tiled=True)  84.6 us
    reduce_scatter x1, waiting for transfers between devices, per_device(): lax.psum_scatter(ffn1_in_g.astype(jnp.bfloat16), 'dp', scatter_dimension=...  63.9 us
  transfers between devices with their start and end apart: 28, of which 26 were waited for; matrix products, arithmetic and copies ran while one was open for 8% of the time, Pallas kernels for 0%

commit v1 on v0

v1 whole, which is shorter than its diff:
```python
import functools
import math

import jax
import jax.numpy as jnp
from jax import lax
from jax.experimental import pallas as pl
from jax.experimental.pallas import tpu as pltpu
from jax.sharding import PartitionSpec as P

HEAD_DIM = 64
BLOCK = 128
LANES = 128
NORM_EPSILON = 1e-05
SCALE = HEAD_DIM ** (-0.5)
F32 = jnp.float32
BF16 = jnp.bfloat16


def product(first, second):
    return jnp.dot(first, second, preferred_element_type=F32)


def left_product(first, second):
    return lax.dot_general(first, second, (((0,), (0,)), ((), ())), preferred_element_type=F32)


def right_product(first, second):
    return lax.dot_general(first, second, (((1,), (1,)), ((), ())), preferred_element_type=F32)


def swish_grad(value):
    sigmoid_out = jax.nn.sigmoid(value)
    return sigmoid_out * (1.0 + value * (1.0 - sigmoid_out))


def norm_forward(value):
    centre = value - jnp.mean(value, -1, keepdims=True)
    inverse = lax.rsqrt(jnp.mean(centre * centre, -1, keepdims=True) + NORM_EPSILON)
    return (centre * inverse, inverse)


def norm_backward(grad_out, normed, inverse, gain):
    scaled = grad_out * gain
    grad_in = inverse * (
        scaled
        - jnp.mean(scaled, -1, keepdims=True)
        - normed * jnp.mean(scaled * normed, -1, keepdims=True)
    )
    return (grad_in, jnp.sum(grad_out * normed, 0))


def bits_of(size):
    return [1 << step for step in range(size.bit_length() - 1)]


def swap(value, axis, bit):
    size = lax.axis_size(axis)
    return lax.ppermute(value, axis, [(rank, rank ^ bit) for rank in range(size)])


def pick(value, index, dim):
    return lax.dynamic_index_in_dim(value, index, dim, keepdims=False)


def gather_rows(share, axis):
    size, rank = lax.axis_size(axis), lax.axis_index(axis)
    held = {0: share}
    for bit in reversed(bits_of(size)):
        for offset, value in list(held.items()):
            held[offset ^ bit] = swap(value, axis, bit)
    rows = share.shape[0]
    whole = jnp.zeros((size * rows,) + share.shape[1:], share.dtype)
    for offset, value in held.items():
        start = (rank ^ offset) * rows
        whole = lax.dynamic_update_slice_in_dim(whole, value, start, 0)
    return whole


def scatter_chunks(chunks, axis):
    rank = lax.axis_index(axis)
    for bit in bits_of(lax.axis_size(axis)):
        count = chunks.shape[0] // 2
        pairs = chunks.reshape((count, 2) + chunks.shape[1:])
        mine = (rank // bit) % 2
        kept, sent = pick(pairs, mine, 1), pick(pairs, 1 - mine, 1)
        got = swap(sent.astype(BF16), axis, bit)
        chunks = kept.astype(F32) + got.astype(F32)
    return chunks[0]


def scatter_rows(value, axis):
    size = lax.axis_size(axis)
    return scatter_chunks(value.reshape((size, value.shape[0] // size) + value.shape[1:]), axis)


def sum_small(value, axis):
    for bit in bits_of(lax.axis_size(axis)):
        value = value + swap(value, axis, bit)
    return value


def merge_moments(count, mean, spread, axis):
    packed = jnp.concatenate([jnp.broadcast_to(count, mean.shape)[None], mean[None], spread[None]])
    for bit in bits_of(lax.axis_size(axis)):
        other = swap(packed, axis, bit)
        n_a, m_a, s_a = packed[0], packed[1], packed[2]
        n_b, m_b, s_b = other[0], other[1], other[2]
        total = n_a + n_b
        safe = jnp.maximum(total, 1.0)
        gap = m_a - m_b
        packed = jnp.stack(
            [
                total,
                (n_a * m_a + n_b * m_b) / safe,
                (s_a + s_b) + gap * gap * (n_a * n_b / safe),
            ]
        )
    return packed[0], packed[1], packed[2]


def trig_tables(frames, features):
    half = features // 2
    blocks = frames // BLOCK
    freqs = jnp.exp(jnp.arange(half).astype(F32) * (-2.0 * math.log(10000.0) / features))

    def both(places):
        angles = places.astype(F32)[:, None] * freqs[None, :]
        return jnp.sin(angles), jnp.cos(angles)

    s_a, c_a = both(jnp.arange(BLOCK // 16) * 16)
    s_b, c_b = both(jnp.arange(16))
    s_a, c_a, s_b, c_b = s_a[:, None], c_a[:, None], s_b[None], c_b[None]
    low_sin = (s_a * c_b + c_a * s_b).reshape(BLOCK, half)
    low_cos = (c_a * c_b - s_a * s_b).reshape(BLOCK, half)
    low = jnp.concatenate([low_sin, low_cos], 1)
    count = -(-blocks // 8) * 8
    s_h, c_h = both((jnp.arange(count) - blocks // 2) * BLOCK)
    high = jnp.concatenate([s_h, c_h], 1)
    high_t = jnp.pad(high, ((0, LANES - count), (0, 0))).T
    return low, high, low.T, high_t


def add_angles(s_h, c_h, s_l, c_l):
    return s_h * c_l + c_h * s_l, c_h * c_l - s_h * s_l


def head_rows(value, heads):
    owner = lax.broadcasted_iota(jnp.int32, value.shape, 0) // HEAD_DIM
    return jnp.concatenate([jnp.where(owner == h, value, 0.0) for h in range(heads)], 1)


def head_lanes(value, heads):
    owner = lax.broadcasted_iota(jnp.int32, value.shape, 1) // HEAD_DIM
    return jnp.concatenate([jnp.where(owner == h, value, 0.0) for h in range(heads)], 0)


def own_rows(value, heads):
    total = None
    for h in range(heads):
        piece = value[:, h * BLOCK : (h + 1) * BLOCK]
        owner = lax.broadcasted_iota(jnp.int32, piece.shape, 0) // HEAD_DIM
        piece = jnp.where(owner == h, piece, 0.0)
        total = piece if total is None else total + piece
    return total


def block_angles(low_t_ref, high_t_ref, block):
    half = low_t_ref.shape[0] // 2
    lane = lax.broadcasted_iota(jnp.int32, high_t_ref.shape, 1)
    column = jnp.sum(jnp.where(lane == block, high_t_ref[...], 0.0), 1, keepdims=True)
    return add_angles(column[:half], column[half:], low_t_ref[:half, :], low_t_ref[half:, :])


def fill_keys(key_ref, low_ref, high_ref, keys_s):
    features = low_ref.shape[1]
    half = features // 2
    width = key_ref.shape[1]
    keys_s[:, :width] = key_ref[...]
    for block in range(key_ref.shape[0] // BLOCK):
        rows = slice(block * BLOCK, (block + 1) * BLOCK)
        high = high_ref[block : block + 1, :]
        sine, cosine = add_angles(
            high[:, :half], high[:, half:], low_ref[:, :half], low_ref[:, half:]
        )
        keys_s[rows, width : width + half] = sine.astype(BF16)
        keys_s[rows, width + half :] = cosine.astype(BF16)


def fill_segments(seg_ref, seg_s):
    for block in range(seg_ref.shape[1] // BLOCK):
        rows = slice(block * BLOCK, (block + 1) * BLOCK)
        seg_s[rows, :] = jnp.broadcast_to(seg_ref[:, rows], (BLOCK, BLOCK)).T


def fill_queries(query_ref, bias_ref, table_ref, sine, cosine, heads, wide_s):
    query = query_ref[...]
    half = sine.shape[0]
    width = query.shape[1]
    q_u = (query + bias_ref[0:1, :]).astype(BF16).astype(F32)
    q_v = (query + bias_ref[1:2, :]).astype(BF16).astype(F32)
    wide_s[:width, :] = head_rows(q_u.T * SCALE, heads).astype(BF16)
    spread = head_rows(q_v.T * SCALE, heads).astype(BF16)
    for_sine = product(table_ref[:half, :], spread)
    for_cosine = product(table_ref[half:, :], spread)
    for h in range(heads):
        lanes = slice(h * BLOCK, (h + 1) * BLOCK)
        u_s, u_c = for_sine[:, lanes], for_cosine[:, lanes]
        wide_s[width : width + half, lanes] = (u_c * sine - u_s * cosine).astype(BF16)
        wide_s[width + half :, lanes] = (u_s * sine + u_c * cosine).astype(BF16)
    return q_u, q_v


def attend_kernel(
    heads,
    pieces,
    query_ref,
    key_ref,
    value_ref,
    seg_ref,
    seg_block_ref,
    bias_ref,
    table_ref,
    low_ref,
    high_ref,
    low_t_ref,
    high_t_ref,
    mixed_ref,
    total_ref,
    keys_s,
    value_t_s,
    seg_s,
    wide_s,
    score_s,
    prob_s,
):
    frames = key_ref.shape[0]
    step = pl.program_id(0)

    @pl.when(step == 0)
    def _():
        fill_keys(key_ref, low_ref, high_ref, keys_s)
        fill_segments(seg_ref, seg_s)
        for block in range(frames // BLOCK):
            rows = slice(block * BLOCK, (block + 1) * BLOCK)
            value_t_s[:, rows] = value_ref[rows, :].astype(F32).T.astype(BF16)

    sine, cosine = block_angles(low_t_ref, high_t_ref, step)
    fill_queries(query_ref, bias_ref, table_ref, sine, cosine, heads, wide_s)
    peaks = [None] * heads
    for rows in pieces:
        scores = product(keys_s[rows, :], wide_s[...])
        linked = seg_s[rows, :] == seg_block_ref[...]
        for h in range(heads):
            lanes = slice(h * BLOCK, (h + 1) * BLOCK)
            part = jnp.where(linked, scores[:, lanes], -1e30)
            score_s[rows, lanes] = part
            peak = jnp.max(part, 0, keepdims=True)
            peaks[h] = peak if peaks[h] is None else jnp.maximum(peaks[h], peak)
    sums = [None] * heads
    for rows in pieces:
        for h in range(heads):
            lanes = slice(h * BLOCK, (h + 1) * BLOCK)
            part = jnp.exp(score_s[rows, lanes] - peaks[h])
            prob_s[rows, lanes] = part.astype(BF16)
            extra = jnp.sum(part, 0, keepdims=True)
            sums[h] = extra if sums[h] is None else sums[h] + extra
    mixed = product(value_t_s[...], prob_s[...])
    mixed = mixed / jnp.concatenate(sums, 1)
    mixed_ref[...] = own_rows(mixed, heads).T.astype(BF16)
    for h in range(heads):
        total_ref[h : h + 1, :] = peaks[h] + jnp.log(sums[h])


def attend_back_kernel(
    heads,
    pieces,
    query_ref,
    key_ref,
    value_ref,
    grad_ref,
    mixed_ref,
    total_ref,
    seg_ref,
    seg_block_ref,
    bias_ref,
    table_ref,
    table_t_ref,
    low_ref,
    high_ref,
    low_t_ref,
    high_t_ref,
    query_g_ref,
    key_g_ref,
    value_g_ref,
    table_g_ref,
    bias_g_ref,
    keys_s,
    keys_t_s,
    seg_s,
    wide_s,
    wide_g_s,
    key_g_s,
    value_g_s,
):
    frames, width = key_ref.shape
    features = low_ref.shape[1]
    half = features // 2
    step = pl.program_id(0)

    @pl.when(step == 0)
    def _():
        fill_keys(key_ref, low_ref, high_ref, keys_s)
        fill_segments(seg_ref, seg_s)
        for block in range(frames // BLOCK):
            rows = slice(block * BLOCK, (block + 1) * BLOCK)
            keys_t_s[:width, rows] = key_ref[rows, :].astype(F32).T.astype(BF16)
            s_j, c_j = block_angles(low_t_ref, high_t_ref, block)
            keys_t_s[width : width + half, rows] = s_j.astype(BF16)
            keys_t_s[width + half :, rows] = c_j.astype(BF16)
        key_g_s[...] = jnp.zeros_like(key_g_s)
        value_g_s[...] = jnp.zeros_like(value_g_s)
        table_g_ref[...] = jnp.zeros_like(table_g_ref)
        bias_g_ref[...] = jnp.zeros_like(bias_g_ref)

    sine, cosine = block_angles(low_t_ref, high_t_ref, step)
    q_u, q_v = fill_queries(query_ref, bias_ref, table_ref, sine, cosine, heads, wide_s)
    grad = grad_ref[...].astype(F32)
    grad_t = grad.T
    weighted = (grad * mixed_ref[...].astype(F32)).T
    owner = lax.broadcasted_iota(jnp.int32, weighted.shape, 0) // HEAD_DIM
    slopes = [
        jnp.sum(jnp.where(owner == h, weighted, 0.0), 0, keepdims=True) for h in range(heads)
    ]
    grad_wide = head_rows(grad_t, heads).astype(BF16)
    grad_tall = head_lanes(grad, heads).astype(BF16)
    query_tall = head_lanes(q_u * SCALE, heads).astype(BF16)
    for number, rows in enumerate(pieces):
        scores = product(keys_s[rows, :], wide_s[...])
        prob_g = product(value_ref[rows, :], grad_wide)
        linked = seg_s[rows, :] == seg_block_ref[...]
        probs, score_gs = [], []
        for h in range(heads):
            lanes = slice(h * BLOCK, (h + 1) * BLOCK)
            part = jnp.where(linked, jnp.exp(scores[:, lanes] - total_ref[h : h + 1, :]), 0.0)
            probs.append(part.astype(BF16))
            score_gs.append((part * (prob_g[:, lanes] - slopes[h])).astype(BF16))
        prob = jnp.concatenate(probs, 1)
        score_g = jnp.concatenate(score_gs, 1)
        value_g_s[rows, :] += product(prob, grad_tall)
        key_g_s[rows, :] += product(score_g, query_tall)
        part = product(keys_t_s[:, rows], score_g)
        if number == 0:
            wide_g_s[...] = part
        else:
            wide_g_s[...] += part
    direct = own_rows(wide_g_s[:width, :], heads) * SCALE
    turned = []
    for h in range(heads):
        lanes = slice(h * BLOCK, (h + 1) * BLOCK)
        d_s = wide_g_s[width : width + half, lanes] * SCALE
        d_c = wide_g_s[width + half :, lanes] * SCALE
        turned.append(
            jnp.concatenate([sine * d_c - cosine * d_s, cosine * d_c + sine * d_s], 0).astype(BF16)
        )
    turned = jnp.concatenate(turned, 1)
    table_g_ref[...] += product(turned, head_lanes(q_v, heads).astype(BF16))
    shifted = own_rows(product(table_t_ref[...], turned), heads)
    query_g_ref[...] = (direct + shifted).T.astype(BF16)
    bias_g_ref[:width, :] += direct
    bias_g_ref[width:, :] += shifted

    @pl.when(step == pl.num_programs(0) - 1)
    def _():
        key_g_ref[...] = key_g_s[...].astype(BF16)
        value_g_ref[...] = value_g_s[...].astype(BF16)


def whole(shape):
    return pl.BlockSpec(shape, lambda i: (0,) * len(shape))


def by_rows(width):
    return pl.BlockSpec((BLOCK, width), lambda i: (i, 0))


def by_lanes(count):
    return pl.BlockSpec((count, BLOCK), lambda i: (0, i))


def cut(frames, sizes):
    pieces, start = [], 0
    for size in sizes:
        if start < frames:
            stop = min(start + size, frames)
            pieces.append(slice(start, stop))
            start = stop
    return pieces


def attend(heads, query, keys, values, segment, bias, table, tables):
    frames, width = keys.shape
    low, high, low_t, high_t = tables
    features = low.shape[1]
    lanes = heads * BLOCK
    pieces = cut(frames, [512, 512] + [640] * frames)
    flops = 2 * frames * frames * lanes // BLOCK * (width + features + width)
    return pl.pallas_call(
        functools.partial(attend_kernel, heads, pieces),
        grid=(frames // BLOCK,),
        in_specs=[
            by_rows(width),
            whole(keys.shape),
            whole(values.shape),
            whole(segment.shape),
            by_lanes(1),
            whole(bias.shape),
            whole(table.shape),
            whole(low.shape),
            whole(high.shape),
            whole(low_t.shape),
            whole(high_t.shape),
        ],
        out_specs=[by_rows(width), by_lanes(heads)],
        out_shape=[
            jax.ShapeDtypeStruct((frames, width), BF16),
            jax.ShapeDtypeStruct((heads, frames), F32),
        ],
        scratch_shapes=[
            pltpu.VMEM((frames, width + features), BF16),
            pltpu.VMEM((width, frames), BF16),
            pltpu.VMEM((frames, BLOCK), F32),
            pltpu.VMEM((width + features, lanes), BF16),
            pltpu.VMEM((frames, lanes), F32),
            pltpu.VMEM((frames, lanes), BF16),
        ],
        cost_estimate=pl.CostEstimate(
            flops=flops, bytes_accessed=8 * frames * width, transcendentals=frames * frames * heads
        ),
        name="attend",
    )(query, keys, values, segment, segment, bias, table, low, high, low_t, high_t)


def attend_back(heads, query, keys, values, grad, mixed, total, segment, bias, table, tables):
    frames, width = keys.shape
    low, high, low_t, high_t = tables
    features = low.shape[1]
    lanes = heads * BLOCK
    pieces = cut(frames, [512, 512] + [640] * frames)
    flops = 2 * frames * frames * lanes // BLOCK * (2 * (width + features) + 3 * width)
    return pl.pallas_call(
        functools.partial(attend_back_kernel, heads, pieces),
        grid=(frames // BLOCK,),
        in_specs=[
            by_rows(width),
            whole(keys.shape),
            whole(values.shape),
            by_rows(width),
            by_rows(width),
            by_lanes(heads),
            whole(segment.shape),
            by_lanes(1),
            whole(bias.shape),
            whole(table.shape),
            whole((width, features)),
            whole(low.shape),
            whole(high.shape),
            whole(low_t.shape),
            whole(high_t.shape),
        ],
        out_specs=[
            by_rows(width),
            whole(keys.shape),
            whole(values.shape),
            whole(table.shape),
            whole((2 * width, BLOCK)),
        ],
        out_shape=[
            jax.ShapeDtypeStruct((frames, width), BF16),
            jax.ShapeDtypeStruct(keys.shape, BF16),
            jax.ShapeDtypeStruct(values.shape, BF16),
            jax.ShapeDtypeStruct(table.shape, F32),
            jax.ShapeDtypeStruct((2 * width, BLOCK), F32),
        ],
        scratch_shapes=[
            pltpu.VMEM((frames, width + features), BF16),
            pltpu.VMEM((width + features, frames), BF16),
            pltpu.VMEM((frames, BLOCK), F32),
            pltpu.VMEM((width + features, lanes), BF16),
            pltpu.VMEM((width + features, lanes), F32),
            pltpu.VMEM((frames, width), F32),
            pltpu.VMEM((frames, width), F32),
        ],
        cost_estimate=pl.CostEstimate(
            flops=flops, bytes_accessed=16 * frames * width, transcendentals=frames * frames * heads
        ),
        name="attend_back",
    )(
        query,
        keys,
        values,
        grad,
        mixed,
        total,
        segment,
        segment,
        bias,
        table,
        table.T,
        low,
        high,
        low_t,
        high_t,
    )


def reach_of(segment, margin):
    frames = segment.shape[0]
    wide = jnp.pad(segment, (margin, margin), constant_values=-2)
    before = sum(
        (wide[margin - d : margin - d + frames] == segment).astype(F32)
        for d in range(1, margin + 1)
    )
    after = sum(
        (wide[margin + d : margin + d + frames] == segment).astype(F32)
        for d in range(1, margin + 1)
    )
    return before, after


EDGE = 16


def conv_kernel(taps, source_ref, weight_ref, before_ref, after_ref, out_ref, wide_s):
    frames, width = source_ref.shape
    margin = (taps - 1) // 2
    edge = jnp.zeros((EDGE, width), F32)
    wide_s[:EDGE, :] = edge
    wide_s[EDGE + frames :, :] = edge
    wide_s[EDGE : EDGE + frames, :] = source_ref[...]

    def one(block, carry):
        base = pl.multiple_of(block * BLOCK, BLOCK)
        before = before_ref[pl.ds(base, BLOCK), :]
        after = after_ref[pl.ds(base, BLOCK), :]
        total = source_ref[pl.ds(base, BLOCK), :] * weight_ref[margin : margin + 1, :]
        for d in range(1, margin + 1):
            prior = wide_s[pl.ds(base + (EDGE - d), BLOCK), :]
            later = wide_s[pl.ds(base + (EDGE + d), BLOCK), :]
            low, high = weight_ref[margin - d : margin - d + 1, :], weight_ref[margin + d : margin + d + 1, :]
            total = total + jnp.where(before >= d, prior, 0.0) * low
            total = total + jnp.where(after >= d, later, 0.0) * high
        out_ref[pl.ds(base, BLOCK), :] = total
        return carry

    lax.fori_loop(0, frames // BLOCK, one, 0)


def conv_back_kernel(
    taps, grad_ref, source_ref, weight_ref, before_ref, after_ref, out_ref, weight_g_ref, grad_s, source_s
):
    frames, width = source_ref.shape
    margin = (taps - 1) // 2
    edge = jnp.zeros((EDGE, width), F32)
    for wide_s, ref in ((grad_s, grad_ref), (source_s, source_ref)):
        wide_s[:EDGE, :] = edge
        wide_s[EDGE + frames :, :] = edge
        wide_s[EDGE : EDGE + frames, :] = ref[...]
    weight_g_ref[...] = jnp.zeros_like(weight_g_ref)

    def fold(value):
        return jnp.sum(value.reshape(BLOCK // 8, 8, width), 0)

    def one(block, carry):
        base = pl.multiple_of(block * BLOCK, BLOCK)
        before = before_ref[pl.ds(base, BLOCK), :]
        after = after_ref[pl.ds(base, BLOCK), :]
        grad = grad_ref[pl.ds(base, BLOCK), :]
        total = grad * weight_ref[margin : margin + 1, :]
        weight_g_ref[8 * margin : 8 * margin + 8, :] += fold(grad * source_ref[pl.ds(base, BLOCK), :])
        for d in range(1, margin + 1):
            for sign, reach in ((-1, before), (1, after)):
                near = margin + sign * d
                far = margin - sign * d
                open_ = reach >= d
                start = base + (EDGE + sign * d)
                total = total + jnp.where(open_, grad_s[pl.ds(start, BLOCK), :], 0.0) * weight_ref[far : far + 1, :]
                weight_g_ref[8 * near : 8 * near + 8, :] += fold(
                    jnp.where(open_, source_s[pl.ds(start, BLOCK), :], 0.0) * grad
                )
        out_ref[pl.ds(base, BLOCK), :] = total
        return carry

    lax.fori_loop(0, frames // BLOCK, one, 0)


def vmem_specs(count):
    return [pl.BlockSpec(memory_space=pltpu.VMEM)] * count


def depthwise(source, weight, before, after):
    frames, width = source.shape
    taps = weight.shape[0]
    return pl.pallas_call(
        functools.partial(conv_kernel, taps),
        in_specs=vmem_specs(4),
        out_specs=pl.BlockSpec(memory_space=pltpu.VMEM),
        out_shape=jax.ShapeDtypeStruct(source.shape, F32),
        scratch_shapes=[pltpu.VMEM((frames + 2 * EDGE, width), F32)],
        cost_estimate=pl.CostEstimate(
            flops=4 * taps * frames * width, bytes_accessed=16 * frames * width, transcendentals=0
        ),
        name="depthwise",
    )(source, weight, before, after)


def depthwise_back(grad, source, weight, before, after):
    frames, width = source.shape
    taps = weight.shape[0]
    out, sums = pl.pallas_call(
        functools.partial(conv_back_kernel, taps),
        in_specs=vmem_specs(5),
        out_specs=vmem_specs(2),
        out_shape=[
            jax.ShapeDtypeStruct(source.shape, F32),
            jax.ShapeDtypeStruct((8 * taps, width), F32),
        ],
        scratch_shapes=[pltpu.VMEM((frames + 2 * EDGE, width), F32)] * 2,
        cost_estimate=pl.CostEstimate(
            flops=8 * taps * frames * width, bytes_accessed=20 * frames * width, transcendentals=0
        ),
        name="depthwise_back",
    )(grad, source, weight, before, after)
    return out, jnp.sum(sums.reshape(taps, 8, width), 1)


def pad_lanes(value):
    width = value.shape[-1]
    extra = -width % LANES
    if not extra:
        return value
    return jnp.pad(value, [(0, 0)] * (value.ndim - 1) + [(0, extra)])


def swish_low(value):
    return (value * jax.nn.sigmoid(value)).astype(BF16)


def per_device(
    layer_input,
    segments,
    out_cotangent,
    norm_gains,
    ffn1_in,
    ffn1_out,
    qkv_weight,
    pos_weight,
    pos_bias,
    out_weight,
    conv_in,
    depth_kernel,
    bn_scale,
    bn_shift,
    conv_out,
    ffn2_in,
    ffn2_out,
):
    rows, frames, features = layer_input.shape
    assert rows == 1 and frames % BLOCK == 0
    segment = segments[0]
    model = lax.axis_size("mp")
    data = lax.axis_size("dp")
    share_rows = frames // model
    share_start = lax.axis_index("mp") * share_rows

    def take_share(value):
        return lax.dynamic_slice_in_dim(value, share_start, share_rows, 0)

    def spread(value):
        return gather_rows(value.astype(BF16), "mp")

    def reduce(value):
        return scatter_rows(value, "mp")

    def by_owner(grad):
        return grad.reshape(data, grad.shape[0] // data, grad.shape[1])

    flat_input = layer_input[0].astype(F32)
    flat_grad = out_cotangent[0].astype(F32)

    normed_all, _ = norm_forward(flat_input)
    hidden_1 = (normed_all * norm_gains[0]).astype(BF16)
    pre_1 = product(hidden_1, ffn1_in)
    active_1 = swish_low(pre_1)
    share_0 = take_share(flat_input)
    share = share_0 + 0.5 * reduce(product(active_1, ffn1_out))
    normed_1, inverse_1 = norm_forward(share_0)

    width = qkv_weight.shape[2]
    heads = width // HEAD_DIM
    tables = trig_tables(frames, features)
    table = jnp.concatenate([pos_weight[0::2], pos_weight[1::2]], 0)
    table_wide = pad_lanes(table)
    bias_wide = pad_lanes(pos_bias)
    segment_row = segment.astype(F32)[None]
    normed_2, inverse_2 = norm_forward(share)
    hidden_2 = spread(normed_2 * norm_gains[1])
    query = pad_lanes(product(hidden_2, qkv_weight[0]))
    keys = pad_lanes(product(hidden_2, qkv_weight[1]).astype(BF16))
    values = pad_lanes(product(hidden_2, qkv_weight[2]).astype(BF16))
    mixed_wide, totals = attend(
        heads, query, keys, values, segment_row, bias_wide, table_wide, tables
    )
    mixed = mixed_wide[:, :width]
    share = share + reduce(product(mixed, out_weight))

    normed_3, inverse_3 = norm_forward(share)
    hidden_3 = spread(normed_3 * norm_gains[2])
    glu_value = product(hidden_3, conv_in[0])
    gate_sig = jax.nn.sigmoid(product(hidden_3, conv_in[1]))
    channels = glu_value * gate_sig
    taps = depth_kernel.shape[0]
    before, after = reach_of(segment, (taps - 1) // 2)
    before = jnp.broadcast_to(before[:, None], channels.shape)
    after = jnp.broadcast_to(after[:, None], channels.shape)
    filtered = depthwise(channels, depth_kernel, before, after)
    valid = (segment >= 0).astype(F32)[:, None]
    count = jnp.sum(valid)
    mean = jnp.sum(valid * filtered, 0) / jnp.maximum(count, 1.0)
    off = filtered - mean
    spread_sum = jnp.sum(valid * off * off, 0)
    counts, bn_mean, bn_square = merge_moments(count, mean, spread_sum, "dp")
    bn_rstd = lax.rsqrt(bn_square / counts + NORM_EPSILON)
    centred = filtered - bn_mean
    bn_normed = centred * bn_rstd
    bn_value = bn_normed * bn_scale + bn_shift
    conv_act = swish_low(bn_value)
    share = share + reduce(product(conv_act, conv_out))

    normed_4, inverse_4 = norm_forward(share)
    hidden_4 = spread(normed_4 * norm_gains[3])
    pre_4 = product(hidden_4, ffn2_in)
    active_4 = swish_low(pre_4)
    share = share + 0.5 * reduce(product(active_4, ffn2_out))
    normed_5, inverse_5 = norm_forward(share)
    layer_output = spread(normed_5 * norm_gains[4])[None]

    gradient, gain_5 = norm_backward(take_share(flat_grad), normed_5, inverse_5, norm_gains[4])

    def ffn_back(gradient, gain, weight_in, weight_out, stored):
        normed, inverse, hidden, pre_act, active = stored
        grad_out = spread(0.5 * gradient)
        grad_pre = (right_product(grad_out, weight_out) * swish_grad(pre_act)).astype(BF16)
        grad_hidden = reduce(right_product(grad_pre, weight_in))
        grad_stream, gain_g = norm_backward(grad_hidden, normed, inverse, gain)
        in_g = scatter_chunks(by_owner(left_product(hidden, grad_pre).astype(BF16)), "dp")
        out_g = scatter_chunks(by_owner(left_product(grad_out, active).astype(BF16)), "dp").T
        return gradient + grad_stream, gain_g, in_g, out_g

    gradient, gain_4, ffn2_in_g, ffn2_out_g = ffn_back(
        gradient, norm_gains[3], ffn2_in, ffn2_out, (normed_4, inverse_4, hidden_4, pre_4, active_4)
    )

    grad_y = spread(gradient)
    conv_out_g = scatter_chunks(by_owner(left_product(grad_y, conv_act).astype(BF16)), "dp").T
    grad_bn = right_product(grad_y, conv_out) * swish_grad(bn_value)
    bn_sums = sum_small(jnp.stack([jnp.sum(grad_bn, 0), jnp.sum(grad_bn * bn_normed, 0)]), "dp")
    shift_g, scale_g = bn_sums[0], bn_sums[1]
    grad_mean = -bn_scale * shift_g * bn_rstd
    grad_var = -0.5 * bn_scale * scale_g * bn_rstd * bn_rstd
    grad_filtered = (
        bn_scale * grad_bn * bn_rstd + valid * (grad_mean + 2.0 * grad_var * centred) / counts
    )
    grad_channels, kernel_local = depthwise_back(
        grad_filtered, channels, depth_kernel, before, after
    )
    grad_value = (grad_channels * gate_sig).astype(BF16)
    grad_gate = (grad_channels * glu_value * gate_sig * (1.0 - gate_sig)).astype(BF16)
    grad_hidden = reduce(right_product(grad_value, conv_in[0]) + right_product(grad_gate, conv_in[1]))
    grad_stream, gain_3 = norm_backward(grad_hidden, normed_3, inverse_3, norm_gains[2])
    gradient = gradient + grad_stream
    conv_in_g = scatter_chunks(
        by_owner(left_product(hidden_3, jnp.concatenate([grad_value, grad_gate], 1)).astype(BF16)), "dp"
    )
    conv_in_g = jnp.stack(jnp.split(conv_in_g, 2, 1))

    grad_y = spread(gradient)
    out_weight_g = scatter_chunks(by_owner(left_product(grad_y, mixed).astype(BF16)), "dp").T
    grad_mixed = pad_lanes(right_product(grad_y, out_weight).astype(BF16))
    query_g, key_g, value_g, table_g, bias_g = attend_back(
        heads, query, keys, values, grad_mixed, mixed_wide, totals, segment_row, bias_wide, table_wide, tables
    )
    query_g, key_g, value_g = query_g[:, :width], key_g[:, :width], value_g[:, :width]
    grad_hidden = reduce(
        right_product(query_g, qkv_weight[0])
        + right_product(key_g, qkv_weight[1])
        + right_product(value_g, qkv_weight[2])
    )
    grad_stream, gain_2 = norm_backward(grad_hidden, normed_2, inverse_2, norm_gains[1])
    gradient = gradient + grad_stream
    qkv_g = scatter_chunks(
        by_owner(left_product(hidden_2, jnp.concatenate([query_g, key_g, value_g], 1)).astype(BF16)), "dp"
    )
    qkv_g = jnp.stack(jnp.split(qkv_g, 3, 1))
    half = features // 2
    table_g = table_g[:, :width]
    pos_weight_g = jnp.stack([table_g[:half], table_g[half:]], 1).reshape(features, width)
    pos_weight_g = scatter_chunks(by_owner(pos_weight_g.astype(BF16)), "dp")
    bias_g = jnp.sum(bias_g, 1).reshape(2, -1)[:, :width]

    gradient, gain_1, ffn1_in_g, ffn1_out_g = ffn_back(
        gradient, norm_gains[0], ffn1_in, ffn1_out, (normed_1, inverse_1, hidden_1, pre_1, active_1)
    )
    input_grad = spread(gradient)[None]

    gains = sum_small(sum_small(jnp.stack([gain_1, gain_2, gain_3, gain_4, gain_5]), "mp"), "dp")
    gain_width = features // data
    gains = lax.dynamic_slice_in_dim(gains, lax.axis_index("dp") * gain_width, gain_width, 1)
    late = sum_small(jnp.concatenate([bias_g, kernel_local], 0), "dp")
    return (
        layer_output,
        input_grad,
        gains,
        ffn1_in_g,
        ffn1_out_g,
        qkv_g,
        pos_weight_g,
        late[:2],
        out_weight_g,
        conv_in_g,
        late[2:],
        scale_g,
        shift_g,
        conv_out_g,
        ffn2_in_g,
        ffn2_out_g,
    )


def solution(mesh):
    placed = (
        P("dp", None, None),
        P("dp", None),
        P("dp", None, None),
        P(),
        P(None, "mp"),
        P("mp", None),
        P(None, None, "mp"),
        P(None, "mp"),
        P(None, "mp"),
        P("mp", None),
        P(None, None, "mp"),
        P(None, "mp"),
        P("mp"),
        P("mp"),
        P("mp", None),
        P(None, "mp"),
        P("mp", None),
    )
    return jax.shard_map(
        per_device,
        mesh=mesh,
        in_specs=placed,
        out_specs=(
            P("dp", None, None),
            P("dp", None, None),
            P(None, "dp"),
            P("dp", "mp"),
            P("mp", "dp"),
            P(None, "dp", "mp"),
            P("dp", "mp"),
            P(None, "mp"),
            P("mp", "dp"),
            P(None, "dp", "mp"),
            P(None, "mp"),
            P("mp"),
            P("mp"),
            P("mp", "dp"),
            P("dp", "mp"),
            P("mp", "dp"),
        ),
        check_vma=False,
    )
```

time: 2530 us -> 513 us (0.20); the launches traced: 2490 us -> 504 us
  local copies, waits for them, and re-layouts: 911 us -> 40.4 us
  waiting for transfers between devices: 986 us -> 159 us
  other arithmetic: 267 us -> 57.1 us
  matrix products: 194 us -> 55.5 us
  blocking collectives: 108 us -> 0 us
  Pallas kernels: 0 us -> 96.2 us
  starting transfers between devices: 2.03 us -> 91.4 us
    reduce_scatter x17 -> x0, waiting for transfers between devices: 732 us -> none  [the longest x4 119 us: reduce_rows(): return lax.psum_scatter(value, 'mp', scatter_dimension=0, tiled=True)]
    rev x2 -> x0, local copies, waits for them, and re-layouts: 326 us -> none  [the longest x1 168 us: rel_shift(): flat_rows.reshape(head_count, frames, 2 * frames)[:, :, :frames][:, :, ::-1]]
    unnamed x483 -> x198, local copies, waits for them, and re-layouts: 272 us -> 10.5 us
    all_gather x10 -> x0, waiting for transfers between devices: 190 us -> none  [the longest x4 84.6 us: spread_rows(): return lax.all_gather(value, 'mp', axis=0, tiled=True)]
    ppermute x0 -> x84, waiting for transfers between devices: none -> 159 us  [swap(): lax.ppermute(value, axis, [(rank, rank ^ bit) for rank in range(size)])]
    reshape x2 -> x0, local copies, waits for them, and re-layouts: 126 us -> none  [the longest x1 63.7 us: rel_shift(): full.reshape(head_count, frames * (2 * frames - 1))]
    dot_general x22 -> x11, matrix products: 142 us -> 21.9 us  [product(): return jnp.dot(first, second, preferred_element_type=F32)]
    scatter-add x28 -> x0, local copies, waits for them, and re-layouts: 109 us -> none  [depthwise_back(): grad_pad.at[:, offset:offset + frames].add(kernel[offset] * masked)]
  transfers between devices with their start and end apart: 28 -> 84, of which waited for: 26 -> 43; matrix products, arithmetic and copies ran while one was open for 8% -> 18% of each run, Pallas kernels for 0% -> 12%
where the time goes in v1:
time: 513 us; the launch traced here: 504 us
  waiting for transfers between devices  159 us (31%)
  Pallas kernels  96.2 us (19%)
  starting transfers between devices  91.4 us (18%)
  other arithmetic  57.1 us (11%)
  matrix products  55.5 us (11%)
  local copies, waits for them, and re-layouts  40.4 us (8%)
    ppermute x84, waiting for transfers between devices, swap(): lax.ppermute(value, axis, [(rank, rank ^ bit) for rank in range(size)])  159 us
    ppermute x84, starting transfers between devices, swap(): lax.ppermute(value, axis, [(rank, rank ^ bit) for rank in range(size)])  91.4 us
    pallas_call x1, Pallas kernels, attend_back(): pl.pallas_call(functools.partial(attend_back_kernel, heads, pieces), grid...  49.4 us
    pallas_call x1, Pallas kernels, attend(): pl.pallas_call(functools.partial(attend_kernel, heads, pieces), grid=(fra...  31.1 us
    dot_general x8, matrix products, left_product(): lax.dot_general(first, second, (((0,), (0,)), ((), ())), preferred_elemen...  22.7 us
    dot_general x11, matrix products, product(): return jnp.dot(first, second, preferred_element_type=F32)  21.9 us
    dynamic_update_slice x27, local copies, waits for them, and re-layouts, gather_rows(): whole = lax.dynamic_update_slice_in_dim(whole, value, start, 0)  11.8 us
    dot_general x11, matrix products, right_product(): lax.dot_general(first, second, (((1,), (1,)), ((), ())), preferred_elemen...  11 us
  transfers between devices with their start and end apart: 84, of which 43 were waited for; matrix products, arithmetic and copies ran while one was open for 18% of the time, Pallas kernels for 12%

profile of v1, /device:TPU:0, one launch (start us, length us, event | category | flops | bytes accessed | tf_op | source)
XLA Modules:
  0.0 503.8 jit_solution(504262868284436576)
XLA Ops:
  4.9 4.5 multiply_convert_fusion.3
  24.0 8.3 %collective-permute-done.1 = bf16[1,416,512]{2,1,0:T(8,128)(2,1)} collective-permute-done((bf16[1,416,512]{2,1,0:T(8,128)(2,1)S(1)}, bf16[1,416,512]{2,1,0:T(8,128)(2,1)}, u32[]{:S(2)}, u32[]{:S(2)}) %collective-permute-start.1) | collective-permute-done | bytes 426016 | tf_op jit(solution)/shard_map/ppermute | solution.py:59
  54.6 31.1 %attend.1 = (bf16[1664,128]{1,0:T(8,128)(2,1)}, f32[2,1664]{1,0:T(2,128)}) custom-call(f32[1664,128]{1,0:T(8,128)} %fusion.57.query_ref, bf16[1664,128]{1,0:T(8,128)(2,1)} %convolution_convert_fusion.2.key_ref, bf16[1664,128]{1,0:T(8,128)(2,1)} %convolution_convert_fusion.1.value_ref, f32[1,1664]{1,0:T(1,128)} %get-tuple-element.113.seg_ref.seg_block_ref, ...), custom_call_target="tpu_custom_call" | custom-call | flops 8506048512 | bytes 1703936 | tf_op jit(solution)/shard_map/attend/pallas_call | solution.py:408
  91.9 10.6 %collective-permute-done.6 = bf16[1,416,512]{2,1,0:T(8,128)(2,1)S(1)} collective-permute-done((bf16[1,416,512]{2,1,0:T(8,128)(2,1)S(1)}, bf16[1,416,512]{2,1,0:T(8,128)(2,1)S(1)}, u32[]{:S(2)}, u32[]{:S(2)}) %collective-permute-start.6) | collective-permute-done | bytes 426016 | tf_op jit(solution)/shard_map/ppermute | solution.py:59
  108.4 8.5 %collective-permute-done.7 = bf16[416,512]{1,0:T(8,128)(2,1)S(1)} collective-permute-done((bf16[416,512]{1,0:T(8,128)(2,1)}, bf16[416,512]{1,0:T(8,128)(2,1)S(1)}, u32[]{:S(2)}, u32[]{:S(2)}) %collective-permute-start.7) | collective-permute-done | bytes 426016 | tf_op jit(solution)/shard_map/ppermute | solution.py:59
  122.3 3.6 fusion.112
  128.4 6.3 %depthwise.1 = f32[1664,128]{1,0:T(8,128)} custom-call(f32[1664,128]{1,0:T(8,128)} %get-tuple-element.127.source_ref, f32[31,128]{1,0:T(8,128)} %weight_ref.3, f32[1664,128]{1,0:T(8,128)} %broadcast_in_dim.25.before_ref, f32[1664,128]{1,0:T(8,128)} %broadcast_in_dim.26.after_ref), custom_call_target="tpu_custom_call" | custom-call | flops 26411008 | bytes 3407872 | tf_op jit(solution)/shard_map/depthwise/pallas_call | solution.py:604
  157.3 10.4 %collective-permute-done.14 = bf16[1,416,512]{2,1,0:T(8,128)(2,1)S(1)} collective-permute-done((bf16[1,416,512]{2,1,0:T(8,128)(2,1)S(1)}, bf16[1,416,512]{2,1,0:T(8,128)(2,1)S(1)}, u32[]{:S(2)}, u32[]{:S(2)}) %collective-permute-start.14) | collective-permute-done | bytes 426016 | tf_op jit(solution)/shard_map/ppermute | solution.py:59
  170.3 9.5 %collective-permute-done.15 = bf16[416,512]{1,0:T(8,128)(2,1)S(1)} collective-permute-done((bf16[416,512]{1,0:T(8,128)(2,1)S(1)}, bf16[416,512]{1,0:T(8,128)(2,1)S(1)}, u32[]{:S(2)}, u32[]{:S(2)}) %collective-permute-start.15) | collective-permute-done | bytes 426016 | tf_op jit(solution)/shard_map/ppermute | solution.py:59
  181.7 3.2 multiply_convert_fusion.2
  190.6 10.4 %collective-permute-done.19 = bf16[1,416,512]{2,1,0:T(8,128)(2,1)S(1)} collective-permute-done((bf16[1,416,512]{2,1,0:T(8,128)(2,1)S(1)}, bf16[1,416,512]{2,1,0:T(8,128)(2,1)S(1)}, u32[]{:S(2)}, u32[]{:S(2)}) %collective-permute-start.19) | collective-permute-done | bytes 426016 | tf_op jit(solution)/shard_map/ppermute | solution.py:59
  209.2 7.6 %collective-permute-done.23 = bf16[416,512]{1,0:T(8,128)(2,1)} collective-permute-done((bf16[416,512]{1,0:T(8,128)(2,1)}, bf16[416,512]{1,0:T(8,128)(2,1)}, u32[]{:S(2)}, u32[]{:S(2)}) %collective-permute-start.23) | collective-permute-done | bytes 426016 | tf_op jit(solution)/shard_map/ppermute | solution.py:59
  216.8 7.4 %collective-permute-done.20 = bf16[416,512]{1,0:T(8,128)(2,1)} collective-permute-done((bf16[416,512]{1,0:T(8,128)(2,1)}, bf16[416,512]{1,0:T(8,128)(2,1)}, u32[]{:S(2)}, u32[]{:S(2)}) %collective-permute-start.20) | collective-permute-done | bytes 426016 | tf_op jit(solution)/shard_map/ppermute | solution.py:59
  230.4 2.7 convolution_convert_fusion.3
  237.6 12.4 %convolution_convert_fusion.4 = bf16[512,512]{1,0:T(8,128)(2,1)S(1)} fusion(bf16[1664,512]{1,0:T(8,128)(2,1)S(1)} %copy-done.16, bf16[1664,512]{1,0:T(8,128)(2,1)S(1)} %multiply_convert_fusion.1), kind=kOutput, calls=%fused_computation.37 | convolution fusion | flops 872677376 | bytes 3932160 | tf_op jit(solution)/shard_map/dot_general | solution.py:25
  253.0 6.3 %collective-permute-done.81 = bf16[4,64,512]{2,1,0:T(8,128)(2,1)S(1)} collective-permute-done((bf16[4,64,512]{2,1,0:T(8,128)(2,1)S(1)}, bf16[4,64,512]{2,1,0:T(8,128)(2,1)S(1)}, u32[]{:S(2)}, u32[]{:S(2)}) %collective-permute-start.81) | collective-permute-done | bytes 262176 | tf_op jit(solution)/shard_map/ppermute | solution.py:59
  266.1 5.8 %collective-permute-done.27 = bf16[1,416,512]{2,1,0:T(8,128)(2,1)S(1)} collective-permute-done((bf16[1,416,512]{2,1,0:T(8,128)(2,1)S(1)}, bf16[1,416,512]{2,1,0:T(8,128)(2,1)S(1)}, u32[]{:S(2)}, u32[]{:S(2)}) %collective-permute-start.27) | collective-permute-done | bytes 426016 | tf_op jit(solution)/shard_map/ppermute | solution.py:59
  277.2 2.6 collective-permute-start.83
  280.4 4.9 collective-permute-done.28
  295.2 2.7 collective-permute-start.33
  303.4 9.5 %depthwise_back.1 = (f32[1664,128]{1,0:T(8,128)}, f32[248,128]{1,0:T(8,128)}) custom-call(f32[1664,128]{1,0:T(8,128)} %divide_add_fusion.grad_ref, f32[1664,128]{1,0:T(8,128)} %get-tuple-element.127.source_ref, f32[31,128]{1,0:T(8,128)} %weight_ref.3, f32[1664,128]{1,0:T(8,128)} %broadcast_in_dim.25.before_ref, f32[1664,128]{1,0:T(8,128)} %broadcast_in_dim.26.after_ref), custom_call_target="tpu_custom_call" | custom-call | flops 52822016 | bytes 4259840 | tf_op jit(solution)/shard_map/depthwise_back/pallas_call | solution.py:620
  321.1 3.4 collective-permute-done.76
  331.6 4.0 collective-permute-done.35
  339.6 6.9 %collective-permute-done.36 = bf16[416,512]{1,0:T(8,128)(2,1)S(1)} collective-permute-done((bf16[416,512]{1,0:T(8,128)(2,1)S(1)}, bf16[416,512]{1,0:T(8,128)(2,1)S(1)}, u32[]{:S(2)}, u32[]{:S(2)}) %collective-permute-start.36) | collective-permute-done | bytes 426016 | tf_op jit(solution)/shard_map/ppermute | solution.py:59
  351.7 49.4 %attend_back.1 = (bf16[1664,128]{1,0:T(8,128)(2,1)}, bf16[1664,128]{1,0:T(8,128)(2,1)}, bf16[1664,128]{1,0:T(8,128)(2,1)}, f32[512,128]{1,0:T(8,128)}, f32[256,128]{1,0:T(8,128)}) custom-call(f32[1664,128]{1,0:T(8,128)} %fusion.57.query_ref, bf16[1664,128]{1,0:T(8,128)(2,1)} %convolution_convert_fusion.2.key_ref, ...), custom_call_target="tpu_custom_call" | custom-call | flops 18429771776 | bytes 3407872 | tf_op jit(solution)/shard_map/attend_back/pallas_call | solution.py:451
  424.8 2.7 collective-permute-start.71
  435.5 3.0 collective-permute-done.40
  442.8 5.8 %collective-permute-done.41 = bf16[416,512]{1,0:T(8,128)(2,1)S(1)} collective-permute-done((bf16[416,512]{1,0:T(8,128)(2,1)S(1)}, bf16[416,512]{1,0:T(8,128)(2,1)S(1)}, u32[]{:S(2)}, u32[]{:S(2)}) %collective-permute-start.41) | collective-permute-done | bytes 426016 | tf_op jit(solution)/shard_map/ppermute | solution.py:59
  460.1 2.7 collective-permute-start.58
  462.8 3.0 collective-permute-done.54
  465.9 2.7 collective-permute-start.55
  474.3 2.8 collective-permute-start.56
  (597 shorter events, 245.1 us)
Async XLA Ops:
  19.1 13.1 %collective-permute-start.1 = (bf16[1,416,512]{2,1,0:T(8,128)(2,1)S(1)}, bf16[1,416,512]{2,1,0:T(8,128)(2,1)}, u32[]{:S(2)}, u32[]{:S(2)}) collective-permute-start(bf16[1,416,512]{2,1,0:T(8,128)(2,1)S(1)} %dynamic-slice_convert_fusion.7), channel_id=1, source_target_pairs={{0,2},{1,3},{2,0},{3,1},{4,6},{5,7},{6,4},{7,5},{8,10},{9,11},{10,... | collective-permute-start | bytes 1277960 | tf_op jit(solution)/shard_map/ppermute | solution.py:59
  35.9 11.9 %collective-permute-start.2 = (bf16[416,512]{1,0:T(8,128)(2,1)}, bf16[416,512]{1,0:T(8,128)(2,1)}, u32[]{:S(2)}, u32[]{:S(2)}) collective-permute-start(bf16[416,512]{1,0:T(8,128)(2,1)} %get-tuple-element.86), channel_id=1, source_target_pairs={{0,2},{1,3},{2,0},{3,1},{4,6},{5,7},{6,4},{7,5},{8,10},{9,11},{10,... | collective-permute-start | bytes 1277960 | tf_op jit(solution)/shard_map/ppermute | solution.py:59
  90.3 12.2 %collective-permute-start.6 = (bf16[1,416,512]{2,1,0:T(8,128)(2,1)S(1)}, bf16[1,416,512]{2,1,0:T(8,128)(2,1)S(1)}, u32[]{:S(2)}, u32[]{:S(2)}) collective-permute-start(bf16[1,416,512]{2,1,0:T(8,128)(2,1)S(1)} %dynamic-slice_convert_fusion.6), channel_id=1, source_target_pairs={{0,2},{1,3},{2,0},{3,1},{4,6},{5,7},{6,4},{7,5},{8,10},{9,11},{10,... | collective-permute-start | bytes 1277960 | tf_op jit(solution)/shard_map/ppermute | solution.py:59
  105.4 11.4 %collective-permute-start.7 = (bf16[416,512]{1,0:T(8,128)(2,1)}, bf16[416,512]{1,0:T(8,128)(2,1)S(1)}, u32[]{:S(2)}, u32[]{:S(2)}) collective-permute-start(bf16[416,512]{1,0:T(8,128)(2,1)} %get-tuple-element.82), channel_id=1, source_target_pairs={{0,2},{1,3},{2,0},{3,1},{4,6},{5,7},{6,4},{7,5},{8,10},{9,11},{10,... | collective-permute-start | bytes 1277960 | tf_op jit(solution)/shard_map/ppermute | solution.py:59
  107.0 10.6 %collective-permute-start.8 = (bf16[416,512]{1,0:T(8,128)(2,1)}, bf16[416,512]{1,0:T(8,128)(2,1)}, u32[]{:S(2)}, u32[]{:S(2)}) collective-permute-start(bf16[416,512]{1,0:T(8,128)(2,1)} %get-tuple-element.82), channel_id=1, source_target_pairs={{0,1},{1,0},{2,3},{3,2},{4,5},{5,4},{6,7},{7,6},{8,9},{9,8},{10,11... | collective-permute-start | bytes 1277960 | tf_op jit(solution)/shard_map/ppermute | solution.py:59
  155.8 11.9 %collective-permute-start.14 = (bf16[1,416,512]{2,1,0:T(8,128)(2,1)S(1)}, bf16[1,416,512]{2,1,0:T(8,128)(2,1)S(1)}, u32[]{:S(2)}, u32[]{:S(2)}) collective-permute-start(bf16[1,416,512]{2,1,0:T(8,128)(2,1)S(1)} %dynamic-slice_convert_fusion.5), channel_id=1, source_target_pairs={{0,2},{1,3},{2,0},{3,1},{4,6},{5,7},{6,4},{7,5},{8,10},{9,11},{10,... | collective-permute-start | bytes 1277960 | tf_op jit(solution)/shard_map/ppermute | solution.py:59
  168.8 11.1 %collective-permute-start.15 = (bf16[416,512]{1,0:T(8,128)(2,1)S(1)}, bf16[416,512]{1,0:T(8,128)(2,1)S(1)}, u32[]{:S(2)}, u32[]{:S(2)}) collective-permute-start(bf16[416,512]{1,0:T(8,128)(2,1)S(1)} %get-tuple-element.74), channel_id=1, source_target_pairs={{0,2},{1,3},{2,0},{3,1},{4,6},{5,7},{6,4},{7,5},{8,10},{9,11},{10,... | collective-permute-start | bytes 1277960 | tf_op jit(solution)/shard_map/ppermute | solution.py:59
  189.1 11.9 %collective-permute-start.19 = (bf16[1,416,512]{2,1,0:T(8,128)(2,1)S(1)}, bf16[1,416,512]{2,1,0:T(8,128)(2,1)S(1)}, u32[]{:S(2)}, u32[]{:S(2)}) collective-permute-start(bf16[1,416,512]{2,1,0:T(8,128)(2,1)S(1)} %dynamic-slice_convert_fusion.4), channel_id=1, source_target_pairs={{0,2},{1,3},{2,0},{3,1},{4,6},{5,7},{6,4},{7,5},{8,10},{9,11},{10,... | collective-permute-start | bytes 1277960 | tf_op jit(solution)/shard_map/ppermute | solution.py:59
  203.8 13.0 %collective-permute-start.23 = (bf16[416,512]{1,0:T(8,128)(2,1)}, bf16[416,512]{1,0:T(8,128)(2,1)}, u32[]{:S(2)}, u32[]{:S(2)}) collective-permute-start(bf16[416,512]{1,0:T(8,128)(2,1)} %get-tuple-element.68), channel_id=1, source_target_pairs={{0,2},{1,3},{2,0},{3,1},{4,6},{5,7},{6,4},{7,5},{8,10},{9,11},{10,... | collective-permute-start | bytes 1277960 | tf_op jit(solution)/shard_map/ppermute | solution.py:59
  207.6 16.7 %collective-permute-start.20 = (bf16[416,512]{1,0:T(8,128)(2,1)}, bf16[416,512]{1,0:T(8,128)(2,1)}, u32[]{:S(2)}, u32[]{:S(2)}) collective-permute-start(bf16[416,512]{1,0:T(8,128)(2,1)} %get-tuple-element.70), channel_id=1, source_target_pairs={{0,2},{1,3},{2,0},{3,1},{4,6},{5,7},{6,4},{7,5},{8,10},{9,11},{10,... | collective-permute-start | bytes 1277960 | tf_op jit(solution)/shard_map/ppermute | solution.py:59
  208.1 19.8 %collective-permute-start.24 = (bf16[416,512]{1,0:T(8,128)(2,1)}, bf16[416,512]{1,0:T(8,128)(2,1)S(1)}, u32[]{:S(2)}, u32[]{:S(2)}) collective-permute-start(bf16[416,512]{1,0:T(8,128)(2,1)} %get-tuple-element.68), channel_id=1, source_target_pairs={{0,1},{1,0},{2,3},{3,2},{4,5},{5,4},{6,7},{7,6},{8,9},{9,8},{10,11... | collective-permute-start | bytes 1277960 | tf_op jit(solution)/shard_map/ppermute | solution.py:59
  208.7 20.1 %collective-permute-start.21 = (bf16[416,512]{1,0:T(8,128)(2,1)}, bf16[416,512]{1,0:T(8,128)(2,1)S(1)}, u32[]{:S(2)}, u32[]{:S(2)}) collective-permute-start(bf16[416,512]{1,0:T(8,128)(2,1)} %get-tuple-element.70), channel_id=1, source_target_pairs={{0,1},{1,0},{2,3},{3,2},{4,5},{5,4},{6,7},{7,6},{8,9},{9,8},{10,11... | collective-permute-start | bytes 1277960 | tf_op jit(solution)/shard_map/ppermute | solution.py:59
  216.8 12.8 %collective-permute-start.25 = (bf16[416,512]{1,0:T(8,128)(2,1)}, bf16[416,512]{1,0:T(8,128)(2,1)S(1)}, u32[]{:S(2)}, u32[]{:S(2)}) collective-permute-start(bf16[416,512]{1,0:T(8,128)(2,1)} %collective-permute-done.23), channel_id=1, source_target_pairs={{0,1},{1,0},{2,3},{3,2},{4,5},{5,4},{6,7},{7,6},{8,9},{9,8},{10,11... | collective-permute-start | bytes 1277960 | tf_op jit(solution)/shard_map/ppermute | solution.py:59
  224.3 27.9 %collective-permute-start.22 = (bf16[416,512]{1,0:T(8,128)(2,1)}, bf16[416,512]{1,0:T(8,128)(2,1)S(1)}, u32[]{:S(2)}, u32[]{:S(2)}) collective-permute-start(bf16[416,512]{1,0:T(8,128)(2,1)} %collective-permute-done.20), channel_id=1, source_target_pairs={{0,1},{1,0},{2,3},{3,2},{4,5},{5,4},{6,7},{7,6},{8,9},{9,8},{10,11... | collective-permute-start | bytes 1277960 | tf_op jit(solution)/shard_map/ppermute | solution.py:59
  236.3 24.7 %collective-permute-start.26 = (bf16[2,416,512]{2,1,0:T(8,128)(2,1)S(1)}, bf16[2,416,512]{2,1,0:T(8,128)(2,1)S(1)}, u32[]{:S(2)}, u32[]{:S(2)}) collective-permute-start(bf16[2,416,512]{2,1,0:T(8,128)(2,1)S(1)} %fusion.17), channel_id=1, source_target_pairs={{0,1},{1,0},{2,3},{3,2},{4,5},{5,4},{6,7},{7,6},{8,9},{9,8},{10,11... | collective-permute-start | bytes 2555912 | tf_op jit(solution)/shard_map/ppermute | solution.py:59
  251.6 12.8 %collective-permute-start.78 = (bf16[4,64,512]{2,1,0:T(8,128)(2,1)S(1)}, bf16[4,64,512]{2,1,0:T(8,128)(2,1)S(1)}, u32[]{:S(2)}, u32[]{:S(2)}) collective-permute-start(bf16[4,64,512]{2,1,0:T(8,128)(2,1)S(1)} %dynamic-slice_bitcast_fusion.1), channel_id=1, source_target_pairs={{0,4},{4,0},{8,12},{12,8},{16,20},{20,16},{24,28},{28,24},{1,5},{5... | collective-permute-start | bytes 786440 | tf_op jit(solution)/shard_map/ppermute | solution.py:59
  261.3 10.6 %collective-permute-start.27 = (bf16[1,416,512]{2,1,0:T(8,128)(2,1)S(1)}, bf16[1,416,512]{2,1,0:T(8,128)(2,1)S(1)}, u32[]{:S(2)}, u32[]{:S(2)}) collective-permute-start(bf16[1,416,512]{2,1,0:T(8,128)(2,1)S(1)} %dynamic-slice_convert_fusion.3), channel_id=1, source_target_pairs={{0,2},{1,3},{2,0},{3,1},{4,6},{5,7},{6,4},{7,5},{8,10},{9,11},{10,... | collective-permute-start | bytes 1277960 | tf_op jit(solution)/shard_map/ppermute | solution.py:59
  264.5 15.4 %collective-permute-start.79 = (bf16[2,64,512]{2,1,0:T(8,128)(2,1)S(1)}, bf16[2,64,512]{2,1,0:T(8,128)(2,1)S(1)}, u32[]{:S(2)}, u32[]{:S(2)}) collective-permute-start(bf16[2,64,512]{2,1,0:T(8,128)(2,1)S(1)} %fusion.42), channel_id=1, source_target_pairs={{0,8},{4,12},{8,0},{12,4},{16,24},{20,28},{24,16},{28,20},{1,9},{5... | collective-permute-start | bytes 393224 | tf_op jit(solution)/shard_map/ppermute | solution.py:59
  275.6 9.7 %collective-permute-start.28 = (bf16[416,512]{1,0:T(8,128)(2,1)S(1)}, bf16[416,512]{1,0:T(8,128)(2,1)S(1)}, u32[]{:S(2)}, u32[]{:S(2)}) collective-permute-start(bf16[416,512]{1,0:T(8,128)(2,1)S(1)} %get-tuple-element.65), channel_id=1, source_target_pairs={{0,2},{1,3},{2,0},{3,1},{4,6},{5,7},{6,4},{7,5},{8,10},{9,11},{10,... | collective-permute-start | bytes 1277960 | tf_op jit(solution)/shard_map/ppermute | solution.py:59
  297.9 21.9 %collective-permute-start.75 = (bf16[4,64,128]{2,1,0:T(8,128)(2,1)S(1)}, bf16[4,64,128]{2,1,0:T(8,128)(2,1)S(1)}, u32[]{:S(2)}, u32[]{:S(2)}) collective-permute-start(bf16[4,64,128]{2,1,0:T(8,128)(2,1)S(1)} %dynamic-slice_bitcast_fusion.6), channel_id=1, source_target_pairs={{0,4},{4,0},{8,12},{12,8},{16,20},{20,16},{24,28},{28,24},{1,5},{5... | collective-permute-start | bytes 196616 | tf_op jit(solution)/shard_map/ppermute | solution.py:59
  325.5 10.2 %collective-permute-start.35 = (bf16[1,416,512]{2,1,0:T(8,128)(2,1)S(1)}, bf16[1,416,512]{2,1,0:T(8,128)(2,1)S(1)}, u32[]{:S(2)}, u32[]{:S(2)}) collective-permute-start(bf16[1,416,512]{2,1,0:T(8,128)(2,1)S(1)} %dynamic-slice_convert_fusion.2), channel_id=1, source_target_pairs={{0,2},{1,3},{2,0},{3,1},{4,6},{5,7},{6,4},{7,5},{8,10},{9,11},{10,... | collective-permute-start | bytes 1277960 | tf_op jit(solution)/shard_map/ppermute | solution.py:59
  327.2 11.7 %collective-permute-start.77 = (bf16[1,64,128]{2,1,0:T(8,128)(2,1)S(1)}, bf16[1,64,128]{2,1,0:T(8,128)(2,1)S(1)}, u32[]{:S(2)}, u32[]{:S(2)}) collective-permute-start(bf16[1,64,128]{2,1,0:T(8,128)(2,1)S(1)} %dynamic-slice_convert_fusion.23), channel_id=1, source_target_pairs={{0,16},{4,20},{8,24},{12,28},{16,0},{20,4},{24,8},{28,12},{1,17},{... | collective-permute-start | bytes 49160 | tf_op jit(solution)/shard_map/ppermute | solution.py:59
  350.6 69.4 %collective-permute-start.69 = (bf16[4,64,128]{2,1,0:T(8,128)(2,1)S(1)}, bf16[4,64,128]{2,1,0:T(8,128)(2,1)}, u32[]{:S(2)}, u32[]{:S(2)}) collective-permute-start(bf16[4,64,128]{2,1,0:T(8,128)(2,1)S(1)} %dynamic-slice_bitcast_fusion.7), channel_id=1, source_target_pairs={{0,4},{4,0},{8,12},{12,8},{16,20},{20,16},{24,28},{28,24},{1,5},{5... | collective-permute-start | bytes 196616 | tf_op jit(solution)/shard_map/ppermute | solution.py:59
  404.4 18.1 %collective-permute-start.63 = (bf16[4,64,128]{2,1,0:T(8,128)(2,1)S(1)}, bf16[4,64,128]{2,1,0:T(8,128)(2,1)S(1)}, u32[]{:S(2)}, u32[]{:S(2)}) collective-permute-start(bf16[4,64,128]{2,1,0:T(8,128)(2,1)S(1)} %dynamic-slice_bitcast_fusion.8), channel_id=1, source_target_pairs={{0,4},{4,0},{8,12},{12,8},{16,20},{20,16},{24,28},{28,24},{1,5},{5... | collective-permute-start | bytes 196616 | tf_op jit(solution)/shard_map/ppermute | solution.py:59
  409.3 20.1 %collective-permute-start.60 = (bf16[4,64,384]{2,1,0:T(8,128)(2,1)S(1)}, bf16[4,64,384]{2,1,0:T(8,128)(2,1)S(1)}, u32[]{:S(2)}, u32[]{:S(2)}) collective-permute-start(bf16[4,64,384]{2,1,0:T(8,128)(2,1)S(1)} %dynamic-slice_bitcast_fusion.4), channel_id=1, source_target_pairs={{0,4},{4,0},{8,12},{12,8},{16,20},{20,16},{24,28},{28,24},{1,5},{5... | collective-permute-start | bytes 589832 | tf_op jit(solution)/shard_map/ppermute | solution.py:59
  416.8 13.0 %collective-permute-start.39 = (bf16[2,416,512]{2,1,0:T(8,128)(2,1)S(1)}, bf16[2,416,512]{2,1,0:T(8,128)(2,1)S(1)}, u32[]{:S(2)}, u32[]{:S(2)}) collective-permute-start(bf16[2,416,512]{2,1,0:T(8,128)(2,1)S(1)} %fusion.19), channel_id=1, source_target_pairs={{0,1},{1,0},{2,3},{3,2},{4,5},{5,4},{6,7},{7,6},{8,9},{9,8},{10,11... | collective-permute-start | bytes 2555912 | tf_op jit(solution)/shard_map/ppermute | solution.py:59
  427.5 14.5 %collective-permute-start.65 = (bf16[1,64,128]{2,1,0:T(8,128)(2,1)S(1)}, bf16[1,64,128]{2,1,0:T(8,128)(2,1)S(1)}, u32[]{:S(2)}, u32[]{:S(2)}) collective-permute-start(bf16[1,64,128]{2,1,0:T(8,128)(2,1)S(1)} %dynamic-slice_convert_fusion.25), channel_id=1, source_target_pairs={{0,16},{4,20},{8,24},{12,28},{16,0},{20,4},{24,8},{28,12},{1,17},{... | collective-permute-start | bytes 49160 | tf_op jit(solution)/shard_map/ppermute | solution.py:59
  458.7 10.0 %collective-permute-start.44 = (bf16[2,416,512]{2,1,0:T(8,128)(2,1)S(1)}, bf16[2,416,512]{2,1,0:T(8,128)(2,1)S(1)}, u32[]{:S(2)}, u32[]{:S(2)}) collective-permute-start(bf16[2,416,512]{2,1,0:T(8,128)(2,1)S(1)} %fusion.20), channel_id=1, source_target_pairs={{0,1},{1,0},{2,3},{3,2},{4,5},{5,4},{6,7},{7,6},{8,9},{9,8},{10,11... | collective-permute-start | bytes 2555912 | tf_op jit(solution)/shard_map/ppermute | solution.py:59
  469.1 10.5 %collective-permute-start.45 = (bf16[1,416,512]{2,1,0:T(8,128)(2,1)S(1)}, bf16[1,416,512]{2,1,0:T(8,128)(2,1)S(1)}, u32[]{:S(2)}, u32[]{:S(2)}) collective-permute-start(bf16[1,416,512]{2,1,0:T(8,128)(2,1)S(1)} %dynamic-slice_convert_fusion), channel_id=1, source_target_pairs={{0,2},{1,3},{2,0},{3,1},{4,6},{5,7},{6,4},{7,5},{8,10},{9,11},{10,... | collective-permute-start | bytes 1277960 | tf_op jit(solution)/shard_map/ppermute | solution.py:59
  471.5 20.1 %collective-permute-start.59 = (bf16[1,64,512]{2,1,0:T(8,128)(2,1)}, bf16[1,64,512]{2,1,0:T(8,128)(2,1)}, u32[]{:S(2)}, u32[]{:S(2)}) collective-permute-start(bf16[1,64,512]{2,1,0:T(8,128)(2,1)} %dynamic-slice_convert_fusion.16), channel_id=1, source_target_pairs={{0,16},{4,20},{8,24},{12,28},{16,0},{20,4},{24,8},{28,12},{1,17},{... | collective-permute-start | bytes 196616 | tf_op jit(solution)/shard_map/ppermute | solution.py:59
  474.3 22.4 %collective-permute-start.56 = (bf16[1,64,512]{2,1,0:T(8,128)(2,1)}, bf16[1,64,512]{2,1,0:T(8,128)(2,1)}, u32[]{:S(2)}, u32[]{:S(2)}) collective-permute-start(bf16[1,64,512]{2,1,0:T(8,128)(2,1)} %dynamic-slice_convert_fusion.17), channel_id=1, source_target_pairs={{0,16},{4,20},{8,24},{12,28},{16,0},{20,4},{24,8},{28,12},{1,17},{... | collective-permute-start | bytes 196616 | tf_op jit(solution)/shard_map/ppermute | solution.py:59
  489.4 11.0 %collective-permute-start.46 = (bf16[416,512]{1,0:T(8,128)(2,1)S(1)}, bf16[416,512]{1,0:T(8,128)(2,1)S(1)}, u32[]{:S(2)}, u32[]{:S(2)}) collective-permute-start(bf16[416,512]{1,0:T(8,128)(2,1)S(1)} %get-tuple-element.52), channel_id=1, source_target_pairs={{0,2},{1,3},{2,0},{3,1},{4,6},{5,7},{6,4},{7,5},{8,10},{9,11},{10,... | collective-permute-start | bytes 1277960 | tf_op jit(solution)/shard_map/ppermute | solution.py:59
  (150 other events, 1432.0 us)
